TPU v7x, 256 devices: a whole 4x4x8 slice. The times are simulated.
256 devices in a mesh: row: 32 (over x, z_hi, y), col: 8 (over z_lo, core).
Axes of the slice: x: 4, y: 4, z: 8 (z_hi: 2, z_lo: 4; z = z_hi * 4 + z_lo), core: 2. Of those that a mesh axis runs over, the one named last changes fastest.
Arguments:
- lanczos_now: float32 [1, 256, 1024], P(None, 'row', 'col'), may hold values from -80 to 80, as said below
- lanczos_prev: float32 [1, 256, 1024], P(None, 'row', 'col'), may hold values from -6 to 6
- beta_prev: float32 [1], replicated, may hold values from 0.3 to 1.5
- valence_energy: float32 [256], P('row'), may hold values from -1.5 to -0.5
- conduction_energy: float32 [1024], P('col'), may hold values from 0.5 to 2.5
- valence_panel: float32 [16384, 256], P(('row', 'col')), may hold values from -0.375 to 0.375
- conduction_panel: float32 [16384, 1024], P(('row', 'col')), may hold values from -0.1875 to 0.1875
- screened_coulomb: float32 [16384, 16384], P('row', 'col'), may hold values from -0.046875 to 0.046875
- bare_coulomb: float32 [16384, 16384], P('row', 'col'), may hold values from -0.046875 to 0.046875
Outputs:
- lanczos_next: float32 [1, 256, 1024], P(None, 'row', 'col')
- coefficients: float32 [1, 2], replicated
Inputs may be any that keep to these rules, and one draw needn't show every extreme that they name: `lanczos_now`: real entries; the vectors of a chain are not normalized.
All inputs are finite; a program needn't handle non-finite values.
Results may differ from a plain program's by a relative error of at most 0.0002.
Values sent between devices are 32-bit elements; how exact they have to be, the bound alone decides.
No kernel may reach another device: no remote copies, remote signals or barrier semaphores. Data moves between devices by JAX's collectives and lax.ppermute only.
A program may use at most 128 MiB of HBM per device.

v0:
```python
import jax
import jax.numpy as jnp
from jax import lax
from jax.experimental import pallas as pl
from jax.experimental.pallas import tpu as pltpu
from jax.sharding import Mesh
from jax.sharding import PartitionSpec as P

V = 256
C = 1024
X, H, Y, L, K = "row_0", "row_1", "row_2", "col_0", "col_1"
SIZES = (4, 2, 4, 4, 2)
AXES = (X, H, Y, L, K)
ROW = (X, H, Y)
COL = (L, K)

f32 = jnp.float32
bf16 = jnp.bfloat16
epsilon = 1e-06
middle_gap = 2.5
inverse_size = 1.0 / (V * C)
SMEM = pl.BlockSpec(memory_space=pltpu.SMEM)
VMEM = pl.BlockSpec(memory_space=pltpu.VMEM)


def copies_to_all(copies, axes):
    return lax.all_to_all(copies, axes, split_axis=0, concat_axis=0, tiled=True)


def from_all(block, axes):
    return copies_to_all(jnp.broadcast_to(block, (lax.axis_size(axes), *block.shape)), axes)


def from_partner(block):
    return lax.ppermute(block, K, [(0, 1), (1, 0)])


def from_next(block, axis, shift):
    return lax.ppermute(block, axis, [((i + shift) % 4, i) for i in range(4)])


def grid_swap(block, flip):
    pairs = []
    for a in range(4):
        for b in range(2):
            for c in range(4):
                for d in range(4):
                    for e in range(2):
                        source = (((a * 2 + b) * 4 + c) * 4 + d) * 2 + e
                        target = (((d * 2 + (e ^ flip)) * 4 + c) * 4 + a) * 2 + b
                        pairs.append((source, target))
    return lax.ppermute(block, AXES, pairs)


def iota(shape, dim):
    return lax.broadcasted_iota(jnp.int32, shape, dim)


def halves(a):
    high = a.astype(bf16)
    return high, (a - high.astype(f32)).astype(bf16)


def product(a, b, dims):
    def one(x, y):
        return lax.dot_general(x, y, (dims, ((), ())), preferred_element_type=f32)

    return one(a[0], b[0]) + (one(a[0], b[1]) + one(a[1], b[0]))


ROWS_BY_ROWS = ((1,), (1,))
PLAIN = ((1,), (0,))
COLUMNS_BY_COLUMNS = ((0,), (0,))


def local_kernel(body, out, flops, scratch=(), grant=8):
    shapes = [pltpu.VMEM(s, f32) for s in out]
    many = len(shapes) > 1

    def call(*args, arguments=()):
        placed = [
            a if a.ndim == 1 else pltpu.with_memory_space_constraint(a, pltpu.VMEM) for a in args
        ] + list(arguments)
        specs = [SMEM if a.ndim == 1 else VMEM for a in placed]
        return pl.pallas_call(
            body,
            out_shape=shapes if many else shapes[0],
            in_specs=specs,
            out_specs=[VMEM] * len(shapes) if many else VMEM,
            scratch_shapes=list(scratch),
            compiler_params=pltpu.CompilerParams(vmem_limit_bytes=grant << 20),
            cost_estimate=pl.CostEstimate(flops=flops, bytes_accessed=1 << 20, transcendentals=0),
        )(*placed)

    return call


def as_column(row, count):
    square = jnp.broadcast_to(row[:, :count], (count, count))
    same = iota((count, count), 0) == iota((count, count), 1)
    return jnp.sum(jnp.where(same, square, 0.0), axis=1, keepdims=True)


def as_row(column, count):
    wide = jnp.broadcast_to(column, (count, V))
    same = iota((count, V), 0) == iota((count, V), 1)
    return jnp.sum(jnp.where(same, wide, 0.0), axis=0, keepdims=True)


def first_kernel(ev_ref, q_ref, p_ref, ec_ref, out_ref):
    ev = jnp.zeros((8, 128), f32)
    for i in range(8):
        ev = jnp.where(iota((8, 128), 0) == i, ev_ref[i], ev)
    gap_q = (ec_ref[...] - ev) * q_ref[...]
    for n in range(8):
        out_ref[n, 0] = q_ref[...]
        out_ref[n, 1] = p_ref[...]
        out_ref[n, 2] = gap_q


def columns_of(pc_ref, which):
    parts = [pc_ref[:, pl.ds(pl.multiple_of((2 * l + which) * 128, 128), 128)] for l in range(4)]
    return halves(jnp.concatenate(parts, axis=1))


def amplitude_kernel(at_ref, own_ref, other_ref, pc_ref, pv_ref, out_ref):
    core = at_ref[0]
    total = jnp.zeros((64, V), f32)
    for ref, which in ((own_ref, core), (other_ref, 1 - core)):
        columns = [
            jnp.concatenate(
                [ref[x * 4 + y, h * 4 + l] for x in range(4) for h in range(2) for y in range(4)],
                axis=0,
            )
            for l in range(4)
        ]
        vectors = halves(jnp.concatenate(columns, axis=1))
        total += product(columns_of(pc_ref, which), vectors, ROWS_BY_ROWS)
    density = as_row(jnp.sum(total * pv_ref[...], axis=1, keepdims=True), 64)
    tail = jnp.where(iota((8, V), 0) == 0, jnp.broadcast_to(density, (8, V)), 0.0)
    for n in range(4):
        out_ref[n, :64] = total
        out_ref[n, 64:] = tail


def density_kernel(at_ref, own_ref, other_ref, out_ref):
    south = at_ref[0] == 0
    for l in range(4):
        own, other = own_ref[l, 64:65, :128], other_ref[l, 64:65, :128]
        first, second = jnp.where(south, own, other), jnp.where(south, other, own)
        out_ref[l : l + 1, :] = first + pltpu.roll(second, 64, 1)


def screened_kernel(at_ref, own_ref, other_ref, *refs):
    a_refs, b_refs, (w_ref, mine_ref, theirs_ref, terms_ref) = refs[:4], refs[4:8], refs[8:]
    core, x, y = at_ref[0], at_ref[1], at_ref[2]
    sides = ((own_ref, core, mine_ref), (other_ref, 1 - core, theirs_ref))
    pairs = [halves(jnp.concatenate([r[l, :64] for l in range(4)], axis=0)) for r, _, _ in sides]
    for t in range(4):
        points = [piece for s in range(4) for piece in (a_refs[t][s], b_refs[s][t])]
        points = halves(jnp.concatenate(points, axis=0))
        for (_, which, out_ref), pair in zip(sides, pairs):
            terms_ref[...] = product(pair, points, ROWS_BY_ROWS)
            for s in range(4):
                at = lax.rem(y + s, 4) * 512 + lax.rem(x + t, 4) * 128
                for l in range(4):
                    rows = pl.ds(pl.multiple_of((2 * l + which) * 64, 64), 64)
                    tile = w_ref[rows, pl.ds(pl.multiple_of(at, 128), 128)]
                    here = (slice(l * 64, l * 64 + 64), slice(s * 128, s * 128 + 128))
                    terms_ref[here] = terms_ref[here] * tile
            done = product(halves(terms_ref[...]), points, PLAIN)
            done = done.reshape(4, 64, V)
            out_ref[...] = done if t == 0 else out_ref[...] + done


def bare_kernel(at_ref, density_ref, b_ref, mine_ref, theirs_ref):
    south = at_ref[0] == 0
    for l in range(4):
        rows = slice(l * 128, l * 128 + 128)
        total = jnp.zeros((128, 128), f32)
        for n in range(16):
            total += b_ref[rows, n * 128 : n * 128 + 128] * density_ref[n : n + 1, :]
        line = jnp.sum(total.T, axis=0, keepdims=True)
        first = jnp.concatenate([line, line], axis=1)
        second = pltpu.roll(first, 192, 1)
        keep = (iota((8, V), 0) == 0) & (iota((8, V), 1) < 64)
        first = jnp.where(keep, jnp.broadcast_to(first, (8, V)), 0.0)
        second = jnp.where(keep, jnp.broadcast_to(second, (8, V)), 0.0)
        mine_ref[l] = jnp.where(south, first, second)
        theirs_ref[l] = jnp.where(south, second, first)


def contribution_kernel(at_ref, sums_ref, pv_ref, pc_ref, own_ref, other_ref):
    core = at_ref[0]
    total = (sums_ref[0] + sums_ref[1]) + (sums_ref[2] + sums_ref[3])
    potential = as_column(total[64:65], 64)
    source = halves(2.0 * potential * pv_ref[...] - total[:64])
    for ref, which in ((other_ref, 1 - core), (own_ref, core)):
        done = product(source, columns_of(pc_ref, which), COLUMNS_BY_COLUMNS)
        for x in range(4):
            for h in range(2):
                for y in range(4):
                    v = ((x * 2 + h) * 4 + y) * 8
                    for l in range(4):
                        ref[x * 4 + y, h * 4 + l] = done[v : v + 8, l * 128 : l * 128 + 128]


def plane_sum_kernel(parts_ref, out_ref):
    for n in range(8):
        total = parts_ref[0, n]
        for i in range(1, 16):
            total += parts_ref[i, n]
        for i in range(8):
            out_ref[i, n] = total


def total_of(a):
    return jnp.sum(jnp.sum(a, axis=0, keepdims=True), axis=1, keepdims=True)


def sums_kernel(beta_ref, parts_ref, piece_ref, shifted_ref, sums_ref):
    beta_prev = beta_ref[0]
    sums = [jnp.zeros((8, 128), f32) for _ in range(4)]
    for n in range(8):
        total = parts_ref[0, n]
        for i in range(1, 8):
            total += parts_ref[i, n]
        q, p = piece_ref[n, 0], piece_ref[n, 1]
        shifted = piece_ref[n, 2] + total - middle_gap * q - beta_prev * p
        shifted_ref[n] = shifted
        sums = [sums[0] + shifted * shifted, sums[1] + shifted * q, sums[2] + q * q, sums[3] + q * p]
    line = jnp.zeros((1, 128), f32)
    for i in range(4):
        line = jnp.where(iota((1, 128), 1) == i, total_of(sums[i]), line)
    for i in range(32):
        sums_ref[i] = line


def last_kernel(beta_ref, at_ref, sums_ref, shifted_ref, q_ref, out_ref, coefficient_ref):
    line = sums_ref[0]
    for i in range(1, 32):
        line += sums_ref[i]
    line = line * inverse_size
    lane = iota((1, 128), 1)
    mean_ww, mean_wq, mean_qq, mean_qp = (
        jnp.sum(jnp.where(lane == i, line, 0.0), axis=1, keepdims=True) for i in range(4)
    )
    mean_qu = mean_wq + middle_gap * mean_qq + beta_ref[0] * mean_qp
    alpha = mean_qu / (mean_qq + epsilon)
    rest = alpha - middle_gap
    mean_rr = mean_ww - 2.0 * rest * mean_wq + rest * rest * mean_qq
    beta = jnp.sqrt(mean_rr + epsilon)
    shifted = shifted_ref[at_ref[3]]
    out_ref[...] = (shifted - rest * q_ref[...]) / beta
    coefficient_ref[...] = jnp.where(iota((1, 2), 1) == 0, alpha, beta)


def per_device(q, p, beta_prev, ev, ec, pv, pc, screened_coulomb, bare_coulomb):
    at = jnp.stack([lax.axis_index(K), lax.axis_index(X), lax.axis_index(Y), lax.axis_index((H, L))])
    at = at.astype(jnp.int32)
    q, p = q[0], p[0]
    copies = local_kernel(first_kernel, [(8, 3, 8, 128)], 1 << 16)(
        arguments=(ev, q, p, ec[None, :])
    )
    piece = copies_to_all(copies, (H, L))
    own_half = from_all(piece[:, 0], (X, Y))
    other_half = from_partner(own_half)

    first, second = grid_swap(pv, 0), grid_swap(pv, 1)
    low = lax.axis_index(H) == 0
    a, b = jnp.where(low, first, second), jnp.where(low, second, first)
    a_parts = jnp.stack([a] + [from_next(a, Y, s) for s in (1, 2, 3)])
    b_parts = jnp.stack([b] + [from_next(b, X, s) for s in (1, 2, 3)])
    a_parts = [a_parts] + [from_next(a_parts, X, s) for s in (1, 2, 3)]
    b_parts = [b_parts] + [from_next(b_parts, Y, s) for s in (1, 2, 3)]

    copies = local_kernel(amplitude_kernel, [(4, 72, V)], 1 << 27)(
        at, own_half, other_half, arguments=(pc, pv)
    )
    own_rows = copies_to_all(copies, L)
    other_rows = from_partner(own_rows)
    row_density = local_kernel(density_kernel, [(4, 128)], 1 << 10)(at, own_rows, other_rows)
    swapped = grid_swap(row_density, 0)
    far_density = from_all(swapped, Y).reshape(16, 128)

    mine, theirs = local_kernel(
        screened_kernel, [(4, 64, V), (4, 64, V)], 3 << 30, [pltpu.VMEM((256, 512), f32)], 24
    )(at, own_rows, other_rows, *a_parts, *b_parts, arguments=(screened_coulomb,))
    mine += from_partner(theirs)
    potential, their_potential = local_kernel(
        bare_kernel, [(4, 8, V), (4, 8, V)], 1 << 26, grant=12
    )(at, far_density, arguments=(bare_coulomb,))
    potential += from_partner(their_potential)
    sums = copies_to_all(jnp.concatenate([mine, potential], axis=1), L)

    own_half, other_half = local_kernel(
        contribution_kernel, [(16, 8, 8, 128)] * 2, 1 << 28
    )(at, sums, arguments=(pv, pc))
    own_half += from_partner(other_half)
    parts = copies_to_all(own_half, (X, Y))
    copies = local_kernel(plane_sum_kernel, [(8, 8, 8, 128)], 1 << 18)(parts)
    parts = copies_to_all(copies, (H, L))

    shifted, sums = local_kernel(
        sums_kernel, [(8, 8, 128), (32, 1, 128)], 1 << 18
    )(beta_prev, parts, piece)
    sums = copies_to_all(sums, (X, Y, K))
    following, coefficients = local_kernel(
        last_kernel, [(8, 128), (1, 2)], 1 << 16
    )(beta_prev, at, sums, shifted, arguments=(q,))
    return following[None], coefficients


def solution(mesh):
    torus = Mesh(mesh.devices.reshape(SIZES), AXES)
    return jax.shard_map(
        per_device,
        mesh=torus,
        in_specs=(
            P(None, ROW, COL),
            P(None, ROW, COL),
            P(),
            P(ROW),
            P(COL),
            P(AXES, None),
            P(AXES, None),
            P(ROW, COL),
            P(ROW, COL),
        ),
        out_specs=(P(None, ROW, COL), P()),
        check_vma=False,
    )
```

profile of v0, /device:TPU:1, one launch (start us, length us, event | category | flops | bytes accessed | tf_op | source)
XLA Modules:
  0.0 181.7 jit_solution(14141344677885723781)
XLA Ops:
  3.9 16.4 %all_to_all.40.piece_ref = f32[8,3,8,128]{3,2,1,0:T(8,128)S(1)} all-to-all(f32[8,3,8,128]{3,2,1,0:T(8,128)S(1)} %shard_map.104), channel_id=1, replica_groups=mesh['row_0'=4,'row_1'=2,'row_2'=4,'col_0'=4,'col_1'=2] {'row_1','col_0'}, dimensions={0} | all-to-all | bytes 196608 | tf_op jit(solution)/shard_map/all_to_all | solution.py:27
  20.4 15.8 %all_to_all.41.own_ref = f32[16,8,8,128]{3,2,1,0:T(8,128)S(1)} all-to-all(f32[16,8,8,128]{3,2,1,0:T(8,128)S(1)} %broadcast_in_dim.13), channel_id=1, replica_groups=mesh['row_0'=4,'row_1'=2,'row_2'=4,'col_0'=4,'col_1'=2] {'row_0','row_2'}, dimensions={0} | all-to-all | bytes 1048576 | tf_op jit(solution)/shard_map/all_to_all | solution.py:27
  36.1 3.2 %collective-permute-start = (f32[16,8,8,128]{3,2,1,0:T(8,128)S(1)}, f32[16,8,8,128]{3,2,1,0:T(8,128)S(1)}, u32[]{:S(2)}, u32[]{:S(2)}) collective-permute-start(f32[16,8,8,128]{3,2,1,0:T(8,128)S(1)} %all_to_all.41.own_ref), channel_id=1, source_target_pairs={{0,1},{1,0},{2,3},{3,2},{4,5},{5,4},{6,7},{7,6},{8,9},{9,8},{10,11... | collective-permute-start | bytes 1572872 | tf_op jit(solution)/shard_map/ppermute | solution.py:35
  39.4 2.8 %collective-permute-start.2 = (f32[64,256]{1,0:T(8,128)}, f32[64,256]{1,0:T(8,128)S(1)}, u32[]{:S(2)}, u32[]{:S(2)}) collective-permute-start(f32[64,256]{1,0:T(8,128)} %pv_ref.3), channel_id=1, source_target_pairs={{0,0},{1,32},{2,64},{3,96},{4,128},{5,160},{6,192},{7,224},{8,8},{... | collective-permute-start | bytes 196616 | tf_op jit(solution)/shard_map/ppermute | solution.py:52
  44.0 1.9 %shard_map.105 = f32[4,72,256]{2,1,0:T(8,128)} custom-call(s32[4]{0:T(128)S(1)} %pad_add_fusion.at_ref, f32[16,8,8,128]{3,2,1,0:T(8,128)S(1)} %all_to_all.41.own_ref, f32[16,8,8,128]{3,2,1,0:T(8,128)S(1)} %collective-permute-done.other_ref, f32[64,1024]{1,0:T(8,128)S(1)} %copy-done.1, f32[64,256]{1,0:T(8,128)S(1)} %copy-done.3), custom_call_target="tpu_custom_call" | custom-call | flops 134217728 | bytes 1048576 | tf_op jit(solution)/shard_map/pallas_call | solution.py:85
  46.0 5.8 %all-to-all-start.2 = ((f32[4,72,256]{2,1,0:T(8,128)}), f32[4,72,256]{2,1,0:T(8,128)S(1)}, u32[]{:S(2)}, u32[]{:S(2)}) async-start(f32[4,72,256]{2,1,0:T(8,128)} %shard_map.105), calls=%async_computation.2 | async-start | bytes 589824 | tf_op jit(solution)/shard_map/all_to_all | solution.py:27
  53.3 1.4 collective-permute-start.4
  54.8 2.5 %collective-permute-done.6 = f32[64,256]{1,0:T(8,128)S(1)} collective-permute-done((f32[64,256]{1,0:T(8,128)S(1)}, f32[64,256]{1,0:T(8,128)S(1)}, u32[]{:S(2)}, u32[]{:S(2)}) %collective-permute-start.6) | collective-permute-done | bytes 65568 | tf_op jit(solution)/shard_map/ppermute | solution.py:39
  57.9 2.3 %collective-permute-start.7 = (f32[4,64,256]{2,1,0:T(8,128)S(1)}, f32[4,64,256]{2,1,0:T(8,128)S(1)}, u32[]{:S(2)}, u32[]{:S(2)}) collective-permute-start(f32[4,64,256]{2,1,0:T(8,128)S(1)} %pad_maximum_fusion.1.refs_0_), channel_id=1, source_target_pairs={{64,0},{128,64},{192,128},{0,192},{65,1},{129,65},{193,129},{1,193... | collective-permute-start | bytes 786440 | tf_op jit(solution)/shard_map/ppermute | solution.py:39
  61.5 1.7 collective-permute-start.11
  63.2 2.1 %collective-permute-start.10 = (f32[64,256]{1,0:T(8,128)S(1)}, f32[64,256]{1,0:T(8,128)S(1)}, u32[]{:S(2)}, u32[]{:S(2)}) collective-permute-start(f32[64,256]{1,0:T(8,128)S(1)} %get-tuple-element.22), channel_id=1, source_target_pairs={{64,0},{128,64},{192,128},{0,192},{65,1},{129,65},{193,129},{1,193... | collective-permute-start | bytes 196616 | tf_op jit(solution)/shard_map/ppermute | solution.py:39
  65.3 6.8 %collective-permute-done.12 = f32[64,256]{1,0:T(8,128)S(1)} collective-permute-done((f32[64,256]{1,0:T(8,128)S(1)}, f32[64,256]{1,0:T(8,128)S(1)}, u32[]{:S(2)}, u32[]{:S(2)}) %collective-permute-start.12) | collective-permute-done | bytes 65568 | tf_op jit(solution)/shard_map/ppermute | solution.py:39
  72.1 1.2 collective-permute-start.1
  73.4 2.9 %collective-permute-start.13 = (f32[4,64,256]{2,1,0:T(8,128)S(1)}, f32[4,64,256]{2,1,0:T(8,128)S(1)}, u32[]{:S(2)}, u32[]{:S(2)}) collective-permute-start(f32[4,64,256]{2,1,0:T(8,128)S(1)} %pad_maximum_fusion.2.refs_4_), channel_id=1, source_target_pairs={{8,0},{16,8},{24,16},{0,24},{9,1},{17,9},{25,17},{1,25},{10,2},{18... | collective-permute-start | bytes 786440 | tf_op jit(solution)/shard_map/ppermute | solution.py:39
  77.0 3.6 %collective-permute-done.9.refs_3_ = f32[4,64,256]{2,1,0:T(8,128)S(1)} collective-permute-done((f32[4,64,256]{2,1,0:T(8,128)S(1)}, f32[4,64,256]{2,1,0:T(8,128)S(1)}, u32[]{:S(2)}, u32[]{:S(2)}) %collective-permute-start.9) | collective-permute-done | bytes 262176 | tf_op jit(solution)/shard_map/ppermute | solution.py:39
  80.6 1.7 collective-permute-done.13.refs_5_
  82.3 1.6 collective-permute-done.14.refs_6_
  83.9 7.7 %collective-permute-done.15.refs_7_ = f32[4,64,256]{2,1,0:T(8,128)S(1)} collective-permute-done((f32[4,64,256]{2,1,0:T(8,128)S(1)}, f32[4,64,256]{2,1,0:T(8,128)S(1)}, u32[]{:S(2)}, u32[]{:S(2)}) %collective-permute-start.15) | collective-permute-done | bytes 262176 | tf_op jit(solution)/shard_map/ppermute | solution.py:39
  91.6 2.2 %copy-done.10 = f32[512,2048]{1,0:T(8,128)S(1)} copy-done((f32[512,2048]{1,0:T(8,128)S(1)}, f32[512,2048]{1,0:T(8,128)}, u32[]{:S(2)}) %copy-start.10) | copy-done | bytes 4194328
  93.8 4.5 %shard_map.106 = (f32[4,64,256]{2,1,0:T(8,128)S(1)}, f32[4,64,256]{2,1,0:T(8,128)S(1)}) custom-call(s32[4]{0:T(128)S(1)} %pad_add_fusion.at_ref, f32[4,72,256]{2,1,0:T(8,128)S(1)} %all-to-all-done.2.own_ref, f32[4,72,256]{2,1,0:T(8,128)S(1)} %collective-permute-done.1.other_ref, f32[4,64,256]{2,1,0:T(8,128)S(1)} %pad_maximum_fusion.1.refs_0_, ...), custom_call_target="tpu_custom_call" | custom-call | flops 3221225472 | bytes 1048576 | tf_op jit(solution)/shard_map/pallas_call | solution.py:85
  99.5 5.4 %collective-permute-start.17 = (f32[4,128]{1,0:T(4,128)S(1)}, f32[4,128]{1,0:T(4,128)S(1)}, u32[]{:S(2)}, u32[]{:S(2)}) collective-permute-start(f32[4,128]{1,0:T(4,128)S(1)} %shard_map.107), channel_id=1, source_target_pairs={{0,0},{1,32},{2,64},{3,96},{4,128},{5,160},{6,192},{7,224},{8,8},{... | collective-permute-start | bytes 6152 | tf_op jit(solution)/shard_map/ppermute | solution.py:52
  104.9 3.4 %collective-permute-done.17 = f32[4,128]{1,0:T(4,128)S(1)} collective-permute-done((f32[4,128]{1,0:T(4,128)S(1)}, f32[4,128]{1,0:T(4,128)S(1)}, u32[]{:S(2)}, u32[]{:S(2)}) %collective-permute-start.17) | collective-permute-done | bytes 2080 | tf_op jit(solution)/shard_map/ppermute | solution.py:52
  108.3 6.5 %all_to_all.42 = f32[4,4,128]{2,1,0:T(4,128)S(1)} all-to-all(f32[4,4,128]{2,1,0:T(4,128)S(1)} %broadcast_in_dim.14), channel_id=1, replica_groups=mesh['row_0'=4,'row_1'=2,'row_2'=4,'col_0'=4,'col_1'=2] {'row_2'}, dimensions={0} | all-to-all | bytes 16384 | tf_op jit(solution)/shard_map/all_to_all | solution.py:27
  115.8 1.2 collective-permute-done.18
  117.1 12.2 %all_to_all.43.sums_ref = f32[4,72,256]{2,1,0:T(8,128)S(1)} all-to-all(f32[4,72,256]{2,1,0:T(8,128)S(1)} %pad_maximum_fusion), channel_id=1, replica_groups=mesh['row_0'=4,'row_1'=2,'row_2'=4,'col_0'=4,'col_1'=2] {'col_0'}, dimensions={0} | all-to-all | bytes 589824 | tf_op jit(solution)/shard_map/all_to_all | solution.py:27
  129.3 1.2 shard_map.109
  130.6 2.0 %collective-permute-start.19 = (f32[16,8,8,128]{3,2,1,0:T(8,128)S(1)}, f32[16,8,8,128]{3,2,1,0:T(8,128)S(1)}, u32[]{:S(2)}, u32[]{:S(2)}) collective-permute-start(f32[16,8,8,128]{3,2,1,0:T(8,128)S(1)} %get-tuple-element.17), channel_id=1, source_target_pairs={{0,1},{1,0},{2,3},{3,2},{4,5},{5,4},{6,7},{7,6},{8,9},{9,8},{10,11... | collective-permute-start | bytes 1572872 | tf_op jit(solution)/shard_map/ppermute | solution.py:35
  132.6 1.5 collective-permute-done.19
  134.2 15.9 %all_to_all.44.parts_ref = f32[16,8,8,128]{3,2,1,0:T(8,128)S(1)} all-to-all(f32[16,8,8,128]{3,2,1,0:T(8,128)S(1)} %add.15), channel_id=1, replica_groups=mesh['row_0'=4,'row_1'=2,'row_2'=4,'col_0'=4,'col_1'=2] {'row_0','row_2'}, dimensions={0} | all-to-all | bytes 1048576 | tf_op jit(solution)/shard_map/all_to_all | solution.py:27
  150.8 5.4 %all-to-all-start.6 = ((f32[8,8,8,128]{3,2,1,0:T(8,128)}), f32[8,8,8,128]{3,2,1,0:T(8,128)S(1)}, u32[]{:S(2)}, u32[]{:S(2)}) async-start(f32[8,8,8,128]{3,2,1,0:T(8,128)} %shard_map.110), calls=%async_computation.6 | async-start | bytes 524288 | tf_op jit(solution)/shard_map/all_to_all | solution.py:27
  156.8 8.8 %all-to-all-done.6.parts_ref = f32[8,8,8,128]{3,2,1,0:T(8,128)S(1)} async-done(((f32[8,8,8,128]{3,2,1,0:T(8,128)}), f32[8,8,8,128]{3,2,1,0:T(8,128)S(1)}, u32[]{:S(2)}, u32[]{:S(2)}) %all-to-all-start.6) | async-done | bytes 262176 | tf_op jit(solution)/shard_map/all_to_all | solution.py:27
  165.7 14.2 %all_to_all.45.sums_ref = f32[32,1,128]{2,1,0:T(1,128)S(1)} all-to-all(f32[32,1,128]{2,1,0:T(1,128)S(1)} %get-tuple-element.18), channel_id=1, replica_groups=mesh['row_0'=4,'row_1'=2,'row_2'=4,'col_0'=4,'col_1'=2] {'row_0','row_2'..., dimensions={0} | all-to-all | bytes 32768 | tf_op jit(solution)/shard_map/all_to_all | solution.py:27
  (62 shorter events, 14.4 us)
Async XLA Ops:
  0.6 0.7 copy-start.5
  1.3 0.7 copy-start.7
  2.0 0.7 copy-start.8
  36.1 6.1 %collective-permute-start = (f32[16,8,8,128]{3,2,1,0:T(8,128)S(1)}, f32[16,8,8,128]{3,2,1,0:T(8,128)S(1)}, u32[]{:S(2)}, u32[]{:S(2)}) collective-permute-start(f32[16,8,8,128]{3,2,1,0:T(8,128)S(1)} %all_to_all.41.own_ref), channel_id=1, source_target_pairs={{0,1},{1,0},{2,3},{3,2},{4,5},{5,4},{6,7},{7,6},{8,9},{9,8},{10,11... | collective-permute-start | bytes 1572872 | tf_op jit(solution)/shard_map/ppermute | solution.py:35
  39.4 12.4 %collective-permute-start.3 = (f32[64,256]{1,0:T(8,128)}, f32[64,256]{1,0:T(8,128)S(1)}, u32[]{:S(2)}, u32[]{:S(2)}) collective-permute-start(f32[64,256]{1,0:T(8,128)} %pv_ref.3), channel_id=1, source_target_pairs={{0,32},{1,0},{2,96},{3,64},{4,160},{5,128},{6,224},{7,192},{8,40},... | collective-permute-start | bytes 196616 | tf_op jit(solution)/shard_map/ppermute | solution.py:52
  39.4 12.4 %collective-permute-start.2 = (f32[64,256]{1,0:T(8,128)}, f32[64,256]{1,0:T(8,128)S(1)}, u32[]{:S(2)}, u32[]{:S(2)}) collective-permute-start(f32[64,256]{1,0:T(8,128)} %pv_ref.3), channel_id=1, source_target_pairs={{0,0},{1,32},{2,64},{3,96},{4,128},{5,160},{6,192},{7,224},{8,8},{... | collective-permute-start | bytes 196616 | tf_op jit(solution)/shard_map/ppermute | solution.py:52
  42.2 1.0 copy-start.1
  43.2 0.8 copy-start.3
  46.0 26.1 %all-to-all-start.2 = ((f32[4,72,256]{2,1,0:T(8,128)}), f32[4,72,256]{2,1,0:T(8,128)S(1)}, u32[]{:S(2)}, u32[]{:S(2)}) async-start(f32[4,72,256]{2,1,0:T(8,128)} %shard_map.105), calls=%async_computation.2 | async-start | bytes 589824 | tf_op jit(solution)/shard_map/all_to_all | solution.py:27
  51.8 5.4 %collective-permute-start.6 = (f32[64,256]{1,0:T(8,128)S(1)}, f32[64,256]{1,0:T(8,128)S(1)}, u32[]{:S(2)}, u32[]{:S(2)}) collective-permute-start(f32[64,256]{1,0:T(8,128)S(1)} %get-tuple-element.23), channel_id=1, source_target_pairs={{24,0},{0,8},{8,16},{16,24},{25,1},{1,9},{9,17},{17,25},{26,2},{2,... | collective-permute-start | bytes 196616 | tf_op jit(solution)/shard_map/ppermute | solution.py:39
  52.2 5.1 %collective-permute-start.5 = (f32[64,256]{1,0:T(8,128)S(1)}, f32[64,256]{1,0:T(8,128)S(1)}, u32[]{:S(2)}, u32[]{:S(2)}) collective-permute-start(f32[64,256]{1,0:T(8,128)S(1)} %get-tuple-element.23), channel_id=1, source_target_pairs={{16,0},{24,8},{0,16},{8,24},{17,1},{25,9},{1,17},{9,25},{18,2},{26... | collective-permute-start | bytes 196616 | tf_op jit(solution)/shard_map/ppermute | solution.py:39
  53.3 4.5 %collective-permute-start.4 = (f32[64,256]{1,0:T(8,128)S(1)}, f32[64,256]{1,0:T(8,128)S(1)}, u32[]{:S(2)}, u32[]{:S(2)}) collective-permute-start(f32[64,256]{1,0:T(8,128)S(1)} %get-tuple-element.23), channel_id=1, source_target_pairs={{8,0},{16,8},{24,16},{0,24},{9,1},{17,9},{25,17},{1,25},{10,2},{18... | collective-permute-start | bytes 196616 | tf_op jit(solution)/shard_map/ppermute | solution.py:39
  57.9 18.4 %collective-permute-start.7 = (f32[4,64,256]{2,1,0:T(8,128)S(1)}, f32[4,64,256]{2,1,0:T(8,128)S(1)}, u32[]{:S(2)}, u32[]{:S(2)}) collective-permute-start(f32[4,64,256]{2,1,0:T(8,128)S(1)} %pad_maximum_fusion.1.refs_0_), channel_id=1, source_target_pairs={{64,0},{128,64},{192,128},{0,192},{65,1},{129,65},{193,129},{1,193... | collective-permute-start | bytes 786440 | tf_op jit(solution)/shard_map/ppermute | solution.py:39
  60.2 16.1 %collective-permute-start.8 = (f32[4,64,256]{2,1,0:T(8,128)S(1)}, f32[4,64,256]{2,1,0:T(8,128)S(1)}, u32[]{:S(2)}, u32[]{:S(2)}) collective-permute-start(f32[4,64,256]{2,1,0:T(8,128)S(1)} %pad_maximum_fusion.1.refs_0_), channel_id=1, source_target_pairs={{128,0},{192,64},{0,128},{64,192},{129,1},{193,65},{1,129},{65,193... | collective-permute-start | bytes 786440 | tf_op jit(solution)/shard_map/ppermute | solution.py:39
  60.7 11.3 %collective-permute-start.12 = (f32[64,256]{1,0:T(8,128)S(1)}, f32[64,256]{1,0:T(8,128)S(1)}, u32[]{:S(2)}, u32[]{:S(2)}) collective-permute-start(f32[64,256]{1,0:T(8,128)S(1)} %get-tuple-element.22), channel_id=1, source_target_pairs={{192,0},{0,64},{64,128},{128,192},{193,1},{1,65},{65,129},{129,193... | collective-permute-start | bytes 196616 | tf_op jit(solution)/shard_map/ppermute | solution.py:39
  61.5 10.6 %collective-permute-start.11 = (f32[64,256]{1,0:T(8,128)S(1)}, f32[64,256]{1,0:T(8,128)S(1)}, u32[]{:S(2)}, u32[]{:S(2)}) collective-permute-start(f32[64,256]{1,0:T(8,128)S(1)} %get-tuple-element.22), channel_id=1, source_target_pairs={{128,0},{192,64},{0,128},{64,192},{129,1},{193,65},{1,129},{65,193... | collective-permute-start | bytes 196616 | tf_op jit(solution)/shard_map/ppermute | solution.py:39
  63.2 10.1 %collective-permute-start.10 = (f32[64,256]{1,0:T(8,128)S(1)}, f32[64,256]{1,0:T(8,128)S(1)}, u32[]{:S(2)}, u32[]{:S(2)}) collective-permute-start(f32[64,256]{1,0:T(8,128)S(1)} %get-tuple-element.22), channel_id=1, source_target_pairs={{64,0},{128,64},{192,128},{0,192},{65,1},{129,65},{193,129},{1,193... | collective-permute-start | bytes 196616 | tf_op jit(solution)/shard_map/ppermute | solution.py:39
  72.1 8.6 %collective-permute-start.9 = (f32[4,64,256]{2,1,0:T(8,128)S(1)}, f32[4,64,256]{2,1,0:T(8,128)S(1)}, u32[]{:S(2)}, u32[]{:S(2)}) collective-permute-start(f32[4,64,256]{2,1,0:T(8,128)S(1)} %pad_maximum_fusion.1.refs_0_), channel_id=1, source_target_pairs={{192,0},{0,64},{64,128},{128,192},{193,1},{1,65},{65,129},{129,193... | collective-permute-start | bytes 786440 | tf_op jit(solution)/shard_map/ppermute | solution.py:39
  72.1 19.5 %collective-permute-start.1 = (f32[4,72,256]{2,1,0:T(8,128)S(1)}, f32[4,72,256]{2,1,0:T(8,128)S(1)}, u32[]{:S(2)}, u32[]{:S(2)}) collective-permute-start(f32[4,72,256]{2,1,0:T(8,128)S(1)} %all-to-all-done.2.own_ref), channel_id=1, source_target_pairs={{0,1},{1,0},{2,3},{3,2},{4,5},{5,4},{6,7},{7,6},{8,9},{9,8},{10,11... | collective-permute-start | bytes 884744 | tf_op jit(solution)/shard_map/ppermute | solution.py:35
  73.3 41.5 %copy-start = (f32[512,2048]{1,0:T(8,128)S(1)}, f32[512,2048]{1,0:T(8,128)}, u32[]{:S(2)}) copy-start(f32[512,2048]{1,0:T(8,128)} %b_ref.1) | copy-start | bytes 12582916
  73.4 8.9 %collective-permute-start.13 = (f32[4,64,256]{2,1,0:T(8,128)S(1)}, f32[4,64,256]{2,1,0:T(8,128)S(1)}, u32[]{:S(2)}, u32[]{:S(2)}) collective-permute-start(f32[4,64,256]{2,1,0:T(8,128)S(1)} %pad_maximum_fusion.2.refs_4_), channel_id=1, source_target_pairs={{8,0},{16,8},{24,16},{0,24},{9,1},{17,9},{25,17},{1,25},{10,2},{18... | collective-permute-start | bytes 786440 | tf_op jit(solution)/shard_map/ppermute | solution.py:39
  76.3 7.6 %collective-permute-start.14 = (f32[4,64,256]{2,1,0:T(8,128)S(1)}, f32[4,64,256]{2,1,0:T(8,128)S(1)}, u32[]{:S(2)}, u32[]{:S(2)}) collective-permute-start(f32[4,64,256]{2,1,0:T(8,128)S(1)} %pad_maximum_fusion.2.refs_4_), channel_id=1, source_target_pairs={{16,0},{24,8},{0,16},{8,24},{17,1},{25,9},{1,17},{9,25},{18,2},{26... | collective-permute-start | bytes 786440 | tf_op jit(solution)/shard_map/ppermute | solution.py:39
  76.3 15.3 %collective-permute-start.15 = (f32[4,64,256]{2,1,0:T(8,128)S(1)}, f32[4,64,256]{2,1,0:T(8,128)S(1)}, u32[]{:S(2)}, u32[]{:S(2)}) collective-permute-start(f32[4,64,256]{2,1,0:T(8,128)S(1)} %pad_maximum_fusion.2.refs_4_), channel_id=1, source_target_pairs={{24,0},{0,8},{8,16},{16,24},{25,1},{1,9},{9,17},{17,25},{26,2},{2,... | collective-permute-start | bytes 786440 | tf_op jit(solution)/shard_map/ppermute | solution.py:39
  91.6 2.2 %copy-start.10 = (f32[512,2048]{1,0:T(8,128)S(1)}, f32[512,2048]{1,0:T(8,128)}, u32[]{:S(2)}) copy-start(f32[512,2048]{1,0:T(8,128)} %refs_8_.1) | copy-start | bytes 12582916
  98.3 31.1 %copy-start.2 = (f32[64,1024]{1,0:T(8,128)S(1)}, f32[64,1024]{1,0:T(8,128)}, u32[]{:S(2)}) copy-start(f32[64,1024]{1,0:T(8,128)} %pc_ref.3) | copy-start | bytes 786436
  98.3 31.1 %copy-start.4 = (f32[64,256]{1,0:T(8,128)S(1)}, f32[64,256]{1,0:T(8,128)}, u32[]{:S(2)}) copy-start(f32[64,256]{1,0:T(8,128)} %pv_ref.3) | copy-start | bytes 196612
  98.3 18.8 %collective-permute-start.16 = (f32[4,64,256]{2,1,0:T(8,128)S(1)}, f32[4,64,256]{2,1,0:T(8,128)S(1)}, u32[]{:S(2)}, u32[]{:S(2)}) collective-permute-start(f32[4,64,256]{2,1,0:T(8,128)S(1)} %get-tuple-element.13), channel_id=1, source_target_pairs={{0,1},{1,0},{2,3},{3,2},{4,5},{5,4},{6,7},{7,6},{8,9},{9,8},{10,11... | collective-permute-start | bytes 786440 | tf_op jit(solution)/shard_map/ppermute | solution.py:35
  99.5 8.8 %collective-permute-start.17 = (f32[4,128]{1,0:T(4,128)S(1)}, f32[4,128]{1,0:T(4,128)S(1)}, u32[]{:S(2)}, u32[]{:S(2)}) collective-permute-start(f32[4,128]{1,0:T(4,128)S(1)} %shard_map.107), channel_id=1, source_target_pairs={{0,0},{1,32},{2,64},{3,96},{4,128},{5,160},{6,192},{7,224},{8,8},{... | collective-permute-start | bytes 6152 | tf_op jit(solution)/shard_map/ppermute | solution.py:52
  115.8 64.2 %copy-start.6 = (f32[1,8,128]{2,1,0:T(8,128)S(1)}, f32[1,8,128]{2,1,0:T(8,128)}, u32[]{:S(2)}) copy-start(f32[1,8,128]{2,1,0:T(8,128)} %param.9) | copy-start | bytes 12292
  115.8 1.3 collective-permute-start.18
  130.6 3.5 %collective-permute-start.19 = (f32[16,8,8,128]{3,2,1,0:T(8,128)S(1)}, f32[16,8,8,128]{3,2,1,0:T(8,128)S(1)}, u32[]{:S(2)}, u32[]{:S(2)}) collective-permute-start(f32[16,8,8,128]{3,2,1,0:T(8,128)S(1)} %get-tuple-element.17), channel_id=1, source_target_pairs={{0,1},{1,0},{2,3},{3,2},{4,5},{5,4},{6,7},{7,6},{8,9},{9,8},{10,11... | collective-permute-start | bytes 1572872 | tf_op jit(solution)/shard_map/ppermute | solution.py:35
  150.8 14.8 %all-to-all-start.6 = ((f32[8,8,8,128]{3,2,1,0:T(8,128)}), f32[8,8,8,128]{3,2,1,0:T(8,128)S(1)}, u32[]{:S(2)}, u32[]{:S(2)}) async-start(f32[8,8,8,128]{3,2,1,0:T(8,128)} %shard_map.110), calls=%async_computation.6 | async-start | bytes 524288 | tf_op jit(solution)/shard_map/all_to_all | solution.py:27
  (1 other events, 0.7 us)
where the time goes:
time: 182 us
  blocking collectives  81 us (45%)
  starting transfers between devices  40.4 us (22%)
  waiting for transfers between devices  39.5 us (22%)
  Pallas kernels  11.3 us (6%)
  local copies, waits for them, and re-layouts  7.85 us (4%)
    all_to_all x6, blocking collectives, copies_to_all(): return lax.all_to_all(copies, axes, split_axis=0, concat_axis=0, tiled=True)  81 us
    ppermute x12, waiting for transfers between devices, from_next(): return lax.ppermute(block, axis, [((i + shift) % 4, i) for i in range(4)])  24.5 us
    ppermute x12, starting transfers between devices, from_next(): return lax.ppermute(block, axis, [((i + shift) % 4, i) for i in range(4)])  14 us
    pallas_call x9, Pallas kernels, call(): pl.pallas_call(body, out_shape=shapes if many else shapes[0], in_specs=sp...  11.3 us
    all_to_all x2, starting transfers between devices, copies_to_all(): return lax.all_to_all(copies, axes, split_axis=0, concat_axis=0, tiled=True)  11.2 us
    all_to_all x2, waiting for transfers between devices, copies_to_all(): return lax.all_to_all(copies, axes, split_axis=0, concat_axis=0, tiled=True)  8.79 us
    ppermute x3, starting transfers between devices, grid_swap(): return lax.ppermute(block, AXES, pairs)  8.15 us
    unnamed x24, local copies, waits for them, and re-layouts  7.79 us
  transfers between devices with their start and end apart: 22, of which 11 were waited for; matrix products, arithmetic and copies ran while one was open for 0% of the time, Pallas kernels for 2%

commit v1 on v0

--- a/solution.py
+++ b/solution.py
@@ -1,3 +1,5 @@
+import functools
+
 import jax
 import jax.numpy as jnp
 from jax import lax
@@ -21,6 +23,7 @@
 inverse_size = 1.0 / (V * C)
 SMEM = pl.BlockSpec(memory_space=pltpu.SMEM)
 VMEM = pl.BlockSpec(memory_space=pltpu.VMEM)
+HBM = pl.BlockSpec(memory_space=pltpu.HBM)
 
 
 def copies_to_all(copies, axes):
@@ -73,15 +76,17 @@
 COLUMNS_BY_COLUMNS = ((0,), (0,))
 
 
-def local_kernel(body, out, flops, scratch=(), grant=8):
-    shapes = [pltpu.VMEM(s, f32) for s in out]
+def local_kernel(body, out, flops, scratch=(), grant=8, placed=True):
+    shapes = [pltpu.VMEM(s, f32) if placed else jax.ShapeDtypeStruct(s, f32) for s in out]
     many = len(shapes) > 1
 
-    def call(*args, arguments=()):
-        placed = [
+    def call(*args, arguments=(), far=()):
+        near = [
             a if a.ndim == 1 else pltpu.with_memory_space_constraint(a, pltpu.VMEM) for a in args
-        ] + list(arguments)
-        specs = [SMEM if a.ndim == 1 else VMEM for a in placed]
+        ]
+        near += list(arguments)
+        far = [pltpu.with_memory_space_constraint(a, pltpu.HBM) for a in far]
+        specs = [SMEM if a.ndim == 1 else VMEM for a in near] + [HBM] * len(far)
         return pl.pallas_call(
             body,
             out_shape=shapes if many else shapes[0],
@@ -90,15 +95,9 @@
             scratch_shapes=list(scratch),
             compiler_params=pltpu.CompilerParams(vmem_limit_bytes=grant << 20),
             cost_estimate=pl.CostEstimate(flops=flops, bytes_accessed=1 << 20, transcendentals=0),
-        )(*placed)
+        )(*near, *far)
 
     return call
-
-
-def as_column(row, count):
-    square = jnp.broadcast_to(row[:, :count], (count, count))
-    same = iota((count, count), 0) == iota((count, count), 1)
-    return jnp.sum(jnp.where(same, square, 0.0), axis=1, keepdims=True)
 
 
 def as_row(column, count):
@@ -107,23 +106,47 @@
     return jnp.sum(jnp.where(same, wide, 0.0), axis=0, keepdims=True)
 
 
-def first_kernel(ev_ref, q_ref, p_ref, ec_ref, out_ref):
+def first_kernel(
+    ev_ref, q_hbm, p_hbm, ec_hbm, pv_hbm, pc_hbm, out_ref, points_ref, q_ref, p_ref, ec_ref, sems
+):
+    pieces = (
+        (q_hbm, q_ref),
+        (p_hbm, p_ref),
+        (ec_hbm, ec_ref),
+        (pv_hbm, points_ref.at[:, :V]),
+        (pc_hbm, points_ref.at[:, V:]),
+    )
+    moves = [pltpu.make_async_copy(a, b, sems.at[n]) for n, (a, b) in enumerate(pieces)]
+    for move in moves:
+        move.start()
     ev = jnp.zeros((8, 128), f32)
     for i in range(8):
         ev = jnp.where(iota((8, 128), 0) == i, ev_ref[i], ev)
+    for move in moves[:3]:
+        move.wait()
     gap_q = (ec_ref[...] - ev) * q_ref[...]
     for n in range(8):
         out_ref[n, 0] = q_ref[...]
         out_ref[n, 1] = p_ref[...]
         out_ref[n, 2] = gap_q
-
-
-def columns_of(pc_ref, which):
-    parts = [pc_ref[:, pl.ds(pl.multiple_of((2 * l + which) * 128, 128), 128)] for l in range(4)]
-    return halves(jnp.concatenate(parts, axis=1))
-
-
-def amplitude_kernel(at_ref, own_ref, other_ref, pc_ref, pv_ref, out_ref):
+    for move in moves[3:]:
+        move.wait()
+
+
+def choose_kernel(at_ref, first_ref, second_ref, a_ref, b_ref):
+    low = at_ref[5] == 0
+    a_ref[...] = jnp.where(low, first_ref[...], second_ref[...])
+    b_ref[...] = jnp.where(low, second_ref[...], first_ref[...])
+
+
+def columns_of(points_ref, which):
+    parts = [
+        points_ref[:, pl.ds(pl.multiple_of(V + (2 * l + which) * 128, 128), 128)] for l in range(4)
+    ]
+    return jnp.concatenate(parts, axis=1)
+
+
+def amplitude_kernel(at_ref, own_ref, other_ref, points_ref, out_ref):
     core = at_ref[0]
     total = jnp.zeros((64, V), f32)
     for ref, which in ((own_ref, core), (other_ref, 1 - core)):
@@ -135,8 +158,8 @@
             for l in range(4)
         ]
         vectors = halves(jnp.concatenate(columns, axis=1))
-        total += product(columns_of(pc_ref, which), vectors, ROWS_BY_ROWS)
-    density = as_row(jnp.sum(total * pv_ref[...], axis=1, keepdims=True), 64)
+        total += product(halves(columns_of(points_ref, which)), vectors, ROWS_BY_ROWS)
+    density = as_row(jnp.sum(total * points_ref[:, :V], axis=1, keepdims=True), 64)
     tail = jnp.where(iota((8, V), 0) == 0, jnp.broadcast_to(density, (8, V)), 0.0)
     for n in range(4):
         out_ref[n, :64] = total
@@ -151,52 +174,75 @@
         out_ref[l : l + 1, :] = first + pltpu.roll(second, 64, 1)
 
 
-def screened_kernel(at_ref, own_ref, other_ref, *refs):
-    a_refs, b_refs, (w_ref, mine_ref, theirs_ref, terms_ref) = refs[:4], refs[4:8], refs[8:]
+def screened_kernel(turns, at_ref, own_ref, other_ref, *refs):
+    a_refs, b_refs, refs = refs[:4], refs[4:8], refs[8:]
+    so_far_ref = None
+    if turns[0] > 0:
+        so_far_ref, refs = refs[0], refs[1:]
     core, x, y = at_ref[0], at_ref[1], at_ref[2]
-    sides = ((own_ref, core, mine_ref), (other_ref, 1 - core, theirs_ref))
-    pairs = [halves(jnp.concatenate([r[l, :64] for l in range(4)], axis=0)) for r, _, _ in sides]
-    for t in range(4):
+    w_hbm, out_ref, w_ref, terms_ref, sems = refs
+    moves = []
+    for n, t in enumerate(turns):
+        for s in range(4):
+            at = pl.multiple_of(lax.rem(y + s, 4) * 512 + lax.rem(x + t, 4) * 128, 128)
+            moves.append(
+                pltpu.make_async_copy(
+                    w_hbm.at[:, pl.ds(at, 128)], w_ref.at[n * 4 + s], sems.at[n * 4 + s]
+                )
+            )
+            moves[-1].start()
+    pairs = [
+        halves(jnp.concatenate([r[l, :64] for l in range(4)], axis=0)) for r in (own_ref, other_ref)
+    ]
+    for n, t in enumerate(turns):
         points = [piece for s in range(4) for piece in (a_refs[t][s], b_refs[s][t])]
         points = halves(jnp.concatenate(points, axis=0))
-        for (_, which, out_ref), pair in zip(sides, pairs):
-            terms_ref[...] = product(pair, points, ROWS_BY_ROWS)
+        for side, which in enumerate((core, 1 - core)):
+            terms_ref[...] = product(pairs[side], points, ROWS_BY_ROWS)
             for s in range(4):
-                at = lax.rem(y + s, 4) * 512 + lax.rem(x + t, 4) * 128
+                if side == 0:
+                    moves[n * 4 + s].wait()
                 for l in range(4):
                     rows = pl.ds(pl.multiple_of((2 * l + which) * 64, 64), 64)
-                    tile = w_ref[rows, pl.ds(pl.multiple_of(at, 128), 128)]
                     here = (slice(l * 64, l * 64 + 64), slice(s * 128, s * 128 + 128))
-                    terms_ref[here] = terms_ref[here] * tile
+                    terms_ref[here] = terms_ref[here] * w_ref[n * 4 + s, rows, :]
             done = product(halves(terms_ref[...]), points, PLAIN)
-            done = done.reshape(4, 64, V)
-            out_ref[...] = done if t == 0 else out_ref[...] + done
-
-
-def bare_kernel(at_ref, density_ref, b_ref, mine_ref, theirs_ref):
-    south = at_ref[0] == 0
-    for l in range(4):
-        rows = slice(l * 128, l * 128 + 128)
-        total = jnp.zeros((128, 128), f32)
-        for n in range(16):
-            total += b_ref[rows, n * 128 : n * 128 + 128] * density_ref[n : n + 1, :]
-        line = jnp.sum(total.T, axis=0, keepdims=True)
-        first = jnp.concatenate([line, line], axis=1)
-        second = pltpu.roll(first, 192, 1)
-        keep = (iota((8, V), 0) == 0) & (iota((8, V), 1) < 64)
-        first = jnp.where(keep, jnp.broadcast_to(first, (8, V)), 0.0)
-        second = jnp.where(keep, jnp.broadcast_to(second, (8, V)), 0.0)
-        mine_ref[l] = jnp.where(south, first, second)
-        theirs_ref[l] = jnp.where(south, second, first)
-
-
-def contribution_kernel(at_ref, sums_ref, pv_ref, pc_ref, own_ref, other_ref):
-    core = at_ref[0]
-    total = (sums_ref[0] + sums_ref[1]) + (sums_ref[2] + sums_ref[3])
-    potential = as_column(total[64:65], 64)
-    source = halves(2.0 * potential * pv_ref[...] - total[:64])
+            mine = slice(side * 256, side * 256 + 256)
+            if n > 0:
+                done += out_ref[mine]
+            elif so_far_ref is not None:
+                done += so_far_ref[mine]
+            out_ref[mine] = done
+
+
+def contribution_kernel(at_ref, density_ref, screened_ref, *refs):
+    points_refs, (b_hbm, own_ref, other_ref, b_ref, sems) = refs[:8], refs[8:]
+    core, z = at_ref[0], at_ref[4]
+    moves = []
+    for side, which in enumerate((core, 1 - core)):
+        for s in range(4):
+            at = pl.multiple_of((2 * lax.rem(z + s, 4) + which) * 64, 64)
+            n = side * 4 + s
+            moves.append(
+                pltpu.make_async_copy(b_hbm.at[pl.ds(at, 64), :], b_ref.at[n], sems.at[n])
+            )
+            moves[-1].start()
+    source = []
+    for side in range(2):
+        for s in range(4):
+            l = lax.rem(z + s, 4)
+            total = jnp.zeros((64, 128), f32)
+            moves[side * 4 + s].wait()
+            for n in range(16):
+                tile = b_ref[side * 4 + s, :, n * 128 : n * 128 + 128]
+                total += tile * density_ref[n : n + 1, :]
+            potential = jnp.sum(total, axis=1, keepdims=True)
+            screened = screened_ref[pl.ds(pl.multiple_of(side * 256 + l * 64, 64), 64), :]
+            source.append(2.0 * potential * points_refs[side * 4 + s][:, :V] - screened)
+    source = halves(jnp.concatenate(source, axis=0))
     for ref, which in ((other_ref, 1 - core), (own_ref, core)):
-        done = product(source, columns_of(pc_ref, which), COLUMNS_BY_COLUMNS)
+        columns = halves(jnp.concatenate([columns_of(r, which) for r in points_refs], axis=0))
+        done = product(source, columns, COLUMNS_BY_COLUMNS)
         for x in range(4):
             for h in range(2):
                 for y in range(4):
@@ -256,46 +302,54 @@
 
 
 def per_device(q, p, beta_prev, ev, ec, pv, pc, screened_coulomb, bare_coulomb):
-    at = jnp.stack([lax.axis_index(K), lax.axis_index(X), lax.axis_index(Y), lax.axis_index((H, L))])
-    at = at.astype(jnp.int32)
+    places = (K, X, Y, (H, L), L, H)
+    at = jnp.stack([lax.axis_index(axis) for axis in places]).astype(jnp.int32)
     q, p = q[0], p[0]
-    copies = local_kernel(first_kernel, [(8, 3, 8, 128)], 1 << 16)(
-        arguments=(ev, q, p, ec[None, :])
-    )
+    small = [pltpu.VMEM((8, 128), f32), pltpu.VMEM((8, 128), f32), pltpu.VMEM((1, 128), f32)]
+    copies, points = local_kernel(
+        first_kernel,
+        [(8, 3, 8, 128), (64, V + C)],
+        1 << 16,
+        small + [pltpu.SemaphoreType.DMA((5,))],
+    )(ev, far=(q, p, ec[None, :], pv, pc))
     piece = copies_to_all(copies, (H, L))
     own_half = from_all(piece[:, 0], (X, Y))
     other_half = from_partner(own_half)
 
+    rows = [points] + [from_next(points, L, s) for s in (1, 2, 3)]
+    rows += [from_partner(r) for r in rows]
+
     first, second = grid_swap(pv, 0), grid_swap(pv, 1)
-    low = lax.axis_index(H) == 0
-    a, b = jnp.where(low, first, second), jnp.where(low, second, first)
+    a, b = local_kernel(choose_kernel, [(64, V)] * 2, 1 << 16)(at, first, second)
     a_parts = jnp.stack([a] + [from_next(a, Y, s) for s in (1, 2, 3)])
     b_parts = jnp.stack([b] + [from_next(b, X, s) for s in (1, 2, 3)])
     a_parts = [a_parts] + [from_next(a_parts, X, s) for s in (1, 2, 3)]
     b_parts = [b_parts] + [from_next(b_parts, Y, s) for s in (1, 2, 3)]
 
-    copies = local_kernel(amplitude_kernel, [(4, 72, V)], 1 << 27)(
-        at, own_half, other_half, arguments=(pc, pv)
-    )
+    copies = local_kernel(amplitude_kernel, [(4, 72, V)], 1 << 27)(at, own_half, other_half, points)
     own_rows = copies_to_all(copies, L)
     other_rows = from_partner(own_rows)
     row_density = local_kernel(density_kernel, [(4, 128)], 1 << 10)(at, own_rows, other_rows)
     swapped = grid_swap(row_density, 0)
     far_density = from_all(swapped, Y).reshape(16, 128)
 
-    mine, theirs = local_kernel(
-        screened_kernel, [(4, 64, V), (4, 64, V)], 3 << 30, [pltpu.VMEM((256, 512), f32)], 24
-    )(at, own_rows, other_rows, *a_parts, *b_parts, arguments=(screened_coulomb,))
-    mine += from_partner(theirs)
-    potential, their_potential = local_kernel(
-        bare_kernel, [(4, 8, V), (4, 8, V)], 1 << 26, grant=12
-    )(at, far_density, arguments=(bare_coulomb,))
-    potential += from_partner(their_potential)
-    sums = copies_to_all(jnp.concatenate([mine, potential], axis=1), L)
+    screened = ()
+    for turns in ((0, 1), (2, 3)):
+        scratch = [pltpu.VMEM((8, 512, 128), f32), pltpu.VMEM((256, 512), f32)]
+        scratch.append(pltpu.SemaphoreType.DMA((8,)))
+        kernel = functools.partial(screened_kernel, turns)
+        done = local_kernel(kernel, [(512, V)], 3 << 29, scratch, 16)(
+            at, own_rows, other_rows, *a_parts, *b_parts, *screened, far=(screened_coulomb,)
+        )
+        screened = (done,)
 
     own_half, other_half = local_kernel(
-        contribution_kernel, [(16, 8, 8, 128)] * 2, 1 << 28
-    )(at, sums, arguments=(pv, pc))
+        contribution_kernel,
+        [(16, 8, 8, 128)] * 2,
+        1 << 29,
+        [pltpu.VMEM((8, 64, 2048), f32), pltpu.SemaphoreType.DMA((8,))],
+        16,
+    )(at, far_density, *screened, *rows, far=(bare_coulomb,))
     own_half += from_partner(other_half)
     parts = copies_to_all(own_half, (X, Y))
     copies = local_kernel(plane_sum_kernel, [(8, 8, 8, 128)], 1 << 18)(parts)
@@ -306,7 +360,7 @@
     )(beta_prev, parts, piece)
     sums = copies_to_all(sums, (X, Y, K))
     following, coefficients = local_kernel(
-        last_kernel, [(8, 128), (1, 2)], 1 << 16
+        last_kernel, [(8, 128), (1, 2)], 1 << 16, placed=False
     )(beta_prev, at, sums, shifted, arguments=(q,))
     return following[None], coefficients
 

time: 182 us -> 183 us (level)
  blocking collectives: 81 us -> 65 us
  starting transfers between devices: 40.4 us -> 56.3 us
  Pallas kernels: 11.3 us -> 20.2 us
  waiting for transfers between devices: 39.5 us -> 35.3 us
  local copies, waits for them, and re-layouts: 7.85 us -> 3.87 us
    all_to_all x6 -> x4, blocking collectives: 81 us -> 65 us  [copies_to_all(): return lax.all_to_all(copies, axes, split_axis=0, concat_axis=0, tiled=True)]
    ppermute x5 -> x7, starting transfers between devices: 7.16 us -> 22.8 us  [from_partner(): return lax.ppermute(block, K, [(0, 1), (1, 0)])]
    ppermute x12 -> x15, waiting for transfers between devices: 24.5 us -> 14.1 us  [from_next(): return lax.ppermute(block, axis, [((i + shift) % 4, i) for i in range(4)])]
    pallas_call x9 -> x10, Pallas kernels: 11.3 us -> 20.2 us  [call(): pl.pallas_call(body, out_shape=shapes if many else shapes[0], in_specs=sp...]
    ppermute x3, waiting for transfers between devices: 3.42 us -> 10.8 us  [grid_swap(): return lax.ppermute(block, AXES, pairs)]
    ppermute x12 -> x15, starting transfers between devices: 14 us -> 19 us  [from_next(): return lax.ppermute(block, axis, [((i + shift) % 4, i) for i in range(4)])]
    unnamed x24 -> x16, local copies, waits for them, and re-layouts: 7.79 us -> 3.14 us
    ppermute x3, starting transfers between devices: 8.15 us -> 4.27 us  [grid_swap(): return lax.ppermute(block, AXES, pairs)]
  transfers between devices with their start and end apart: 22 -> 28, of which waited for: 11 -> 9; matrix products, arithmetic and copies ran while one was open for 0% -> 0% of each run, Pallas kernels for 2% -> 6%
where the time goes in v1:
time: 183 us; the launch traced here: 182 us
  blocking collectives  65 us (36%)
  starting transfers between devices  56.3 us (31%)
  waiting for transfers between devices  35.3 us (19%)
  Pallas kernels  20.2 us (11%)
  local copies, waits for them, and re-layouts  3.87 us (2%)
    all_to_all x4, blocking collectives, copies_to_all(): return lax.all_to_all(copies, axes, split_axis=0, concat_axis=0, tiled=True)  65 us
    ppermute x7, starting transfers between devices, from_partner(): return lax.ppermute(block, K, [(0, 1), (1, 0)])  22.8 us
    pallas_call x10, Pallas kernels, call(): pl.pallas_call(body, out_shape=shapes if many else shapes[0], in_specs=sp...  20.2 us
    ppermute x15, starting transfers between devices, from_next(): return lax.ppermute(block, axis, [((i + shift) % 4, i) for i in range(4)])  19 us
    ppermute x15, waiting for transfers between devices, from_next(): return lax.ppermute(block, axis, [((i + shift) % 4, i) for i in range(4)])  14.1 us
    ppermute x3, waiting for transfers between devices, grid_swap(): return lax.ppermute(block, AXES, pairs)  10.8 us
    all_to_all x3, starting transfers between devices, copies_to_all(): return lax.all_to_all(copies, axes, split_axis=0, concat_axis=0, tiled=True)  10.1 us
    all_to_all x3, waiting for transfers between devices, copies_to_all(): return lax.all_to_all(copies, axes, split_axis=0, concat_axis=0, tiled=True)  8.47 us
  transfers between devices with their start and end apart: 28, of which 9 were waited for; matrix products, arithmetic and copies ran while one was open for 0% of the time, Pallas kernels for 6%

profile of v1, /device:TPU:1, one launch (start us, length us, event | category | flops | bytes accessed | tf_op | source)
XLA Modules:
  0.0 182.3 jit_solution(15417821916119344489)
XLA Ops:
  1.3 1.6 shard_map.104
  2.9 16.4 %all_to_all.35.piece_ref = f32[8,3,8,128]{3,2,1,0:T(8,128)S(1)} all-to-all(f32[8,3,8,128]{3,2,1,0:T(8,128)S(1)} %get-tuple-element.12), channel_id=1, replica_groups=mesh['row_0'=4,'row_1'=2,'row_2'=4,'col_0'=4,'col_1'=2] {'row_1','col_0'}, dimensions={0} | all-to-all | bytes 196608 | tf_op jit(solution)/shard_map/all_to_all | solution.py:30
  20.0 15.7 %all_to_all.36.own_ref = f32[16,8,8,128]{3,2,1,0:T(8,128)S(1)} all-to-all(f32[16,8,8,128]{3,2,1,0:T(8,128)S(1)} %broadcast_in_dim.13), channel_id=1, replica_groups=mesh['row_0'=4,'row_1'=2,'row_2'=4,'col_0'=4,'col_1'=2] {'row_0','row_2'}, dimensions={0} | all-to-all | bytes 1048576 | tf_op jit(solution)/shard_map/all_to_all | solution.py:30
  35.7 3.2 %collective-permute-start = (f32[16,8,8,128]{3,2,1,0:T(8,128)S(1)}, f32[16,8,8,128]{3,2,1,0:T(8,128)S(1)}, u32[]{:S(2)}, u32[]{:S(2)}) collective-permute-start(f32[16,8,8,128]{3,2,1,0:T(8,128)S(1)} %all_to_all.36.own_ref), channel_id=1, source_target_pairs={{0,1},{1,0},{2,3},{3,2},{4,5},{5,4},{6,7},{7,6},{8,9},{9,8},{10,11... | collective-permute-start | bytes 1572872 | tf_op jit(solution)/shard_map/ppermute | solution.py:38
  39.0 2.3 %collective-permute-start.3 = (f32[64,256]{1,0:T(8,128)}, f32[64,256]{1,0:T(8,128)S(1)}, u32[]{:S(2)}, u32[]{:S(2)}) collective-permute-start(f32[64,256]{1,0:T(8,128)} %pv_hbm.1), channel_id=1, source_target_pairs={{0,0},{1,32},{2,64},{3,96},{4,128},{5,160},{6,192},{7,224},{8,8},{... | collective-permute-start | bytes 196616 | tf_op jit(solution)/shard_map/ppermute | solution.py:55
  41.4 8.1 %collective-permute-done.3.first_ref = f32[64,256]{1,0:T(8,128)S(1)} collective-permute-done((f32[64,256]{1,0:T(8,128)}, f32[64,256]{1,0:T(8,128)S(1)}, u32[]{:S(2)}, u32[]{:S(2)}) %collective-permute-start.3) | collective-permute-done | bytes 65568 | tf_op jit(solution)/shard_map/ppermute | solution.py:55
  50.4 1.8 collective-permute-start.6
  52.2 3.9 %collective-permute-start.17 = (f32[64,1280]{1,0:T(8,128)S(1)}, f32[64,1280]{1,0:T(8,128)}, u32[]{:S(2)}, u32[]{:S(2)}) collective-permute-start(f32[64,1280]{1,0:T(8,128)S(1)} %get-tuple-element.13.points_ref.refs_0_), channel_id=1, source_target_pairs={{2,0},{4,2},{6,4},{0,6},{3,1},{5,3},{7,5},{1,7},{10,8},{12,10},{14... | collective-permute-start | bytes 983048 | tf_op jit(solution)/shard_map/ppermute | solution.py:42
  56.1 1.9 %shard_map.105 = f32[4,72,256]{2,1,0:T(8,128)} custom-call(s32[6]{0:T(128)S(1)} %stack.57.at_ref, f32[16,8,8,128]{3,2,1,0:T(8,128)S(1)} %all_to_all.36.own_ref, f32[16,8,8,128]{3,2,1,0:T(8,128)S(1)} %collective-permute-done.other_ref, f32[64,1280]{1,0:T(8,128)S(1)} %get-tuple-element.13.points_ref.refs_0_), custom_call_target="tpu_custom_call" | custom-call | flops 134217728 | bytes 1048576 | tf_op jit(solution)/shard_map/pallas_call | solution.py:90
  58.0 3.5 %all-to-all-start.2 = ((f32[4,72,256]{2,1,0:T(8,128)}), f32[4,72,256]{2,1,0:T(8,128)S(1)}, u32[]{:S(2)}, u32[]{:S(2)}) async-start(f32[4,72,256]{2,1,0:T(8,128)} %shard_map.105), calls=%async_computation.2 | async-start | bytes 589824 | tf_op jit(solution)/shard_map/all_to_all | solution.py:30
  61.5 2.3 %collective-permute-start.18 = (f32[64,1280]{1,0:T(8,128)S(1)}, f32[64,1280]{1,0:T(8,128)}, u32[]{:S(2)}, u32[]{:S(2)}) collective-permute-start(f32[64,1280]{1,0:T(8,128)S(1)} %get-tuple-element.13.points_ref.refs_0_), channel_id=1, source_target_pairs={{4,0},{6,2},{0,4},{2,6},{5,1},{7,3},{1,5},{3,7},{12,8},{14,10},{8,... | collective-permute-start | bytes 983048 | tf_op jit(solution)/shard_map/ppermute | solution.py:42
  65.4 1.8 %collective-permute-done.11 = f32[64,256]{1,0:T(8,128)S(1)} collective-permute-done((f32[64,256]{1,0:T(8,128)S(1)}, f32[64,256]{1,0:T(8,128)S(1)}, u32[]{:S(2)}, u32[]{:S(2)}) %collective-permute-start.11) | collective-permute-done | bytes 65568 | tf_op jit(solution)/shard_map/ppermute | solution.py:42
  67.2 1.2 collective-permute-start.19
  69.9 2.8 %collective-permute-start.14 = (f32[4,64,256]{2,1,0:T(8,128)S(1)}, f32[4,64,256]{2,1,0:T(8,128)S(1)}, u32[]{:S(2)}, u32[]{:S(2)}) collective-permute-start(f32[4,64,256]{2,1,0:T(8,128)S(1)} %pad_maximum_fusion.1.refs_4_), channel_id=1, source_target_pairs={{8,0},{16,8},{24,16},{0,24},{9,1},{17,9},{25,17},{1,25},{10,2},{18... | collective-permute-start | bytes 786440 | tf_op jit(solution)/shard_map/ppermute | solution.py:42
  72.7 14.2 %collective-permute-start.1 = (f32[4,72,256]{2,1,0:T(8,128)S(1)}, f32[4,72,256]{2,1,0:T(8,128)S(1)}, u32[]{:S(2)}, u32[]{:S(2)}) collective-permute-start(f32[4,72,256]{2,1,0:T(8,128)S(1)} %all-to-all-done.2.own_ref), channel_id=1, source_target_pairs={{0,1},{1,0},{2,3},{3,2},{4,5},{5,4},{6,7},{7,6},{8,9},{9,8},{10,11... | collective-permute-start | bytes 884744 | tf_op jit(solution)/shard_map/ppermute | solution.py:38
  86.9 4.9 %collective-permute-done.18.refs_2_ = f32[64,1280]{1,0:T(8,128)} collective-permute-done((f32[64,1280]{1,0:T(8,128)S(1)}, f32[64,1280]{1,0:T(8,128)}, u32[]{:S(2)}, u32[]{:S(2)}) %collective-permute-start.18) | collective-permute-done | bytes 327712 | tf_op jit(solution)/shard_map/ppermute | solution.py:42
  91.8 2.9 %collective-permute-start.15 = (f32[4,64,256]{2,1,0:T(8,128)S(1)}, f32[4,64,256]{2,1,0:T(8,128)S(1)}, u32[]{:S(2)}, u32[]{:S(2)}) collective-permute-start(f32[4,64,256]{2,1,0:T(8,128)S(1)} %pad_maximum_fusion.1.refs_4_), channel_id=1, source_target_pairs={{16,0},{24,8},{0,16},{8,24},{17,1},{25,9},{1,17},{9,25},{18,2},{26... | collective-permute-start | bytes 786440 | tf_op jit(solution)/shard_map/ppermute | solution.py:42
  96.1 3.8 %collective-permute-done.15.refs_6_ = f32[4,64,256]{2,1,0:T(8,128)S(1)} collective-permute-done((f32[4,64,256]{2,1,0:T(8,128)S(1)}, f32[4,64,256]{2,1,0:T(8,128)S(1)}, u32[]{:S(2)}, u32[]{:S(2)}) %collective-permute-start.15) | collective-permute-done | bytes 262176 | tf_op jit(solution)/shard_map/ppermute | solution.py:42
  99.9 3.9 %collective-permute-start.20 = (f32[64,1280]{1,0:T(8,128)S(1)}, f32[64,1280]{1,0:T(8,128)}, u32[]{:S(2)}, u32[]{:S(2)}) collective-permute-start(f32[64,1280]{1,0:T(8,128)S(1)} %get-tuple-element.13.points_ref.refs_0_), channel_id=1, source_target_pairs={{0,1},{1,0},{2,3},{3,2},{4,5},{5,4},{6,7},{7,6},{8,9},{9,8},{10,11... | collective-permute-start | bytes 983048 | tf_op jit(solution)/shard_map/ppermute | solution.py:38
  103.8 3.0 %collective-permute-done.16.refs_7_ = f32[4,64,256]{2,1,0:T(8,128)S(1)} collective-permute-done((f32[4,64,256]{2,1,0:T(8,128)S(1)}, f32[4,64,256]{2,1,0:T(8,128)S(1)}, u32[]{:S(2)}, u32[]{:S(2)}) %collective-permute-start.16) | collective-permute-done | bytes 262176 | tf_op jit(solution)/shard_map/ppermute | solution.py:42
  108.8 1.9 %collective-permute-start.2 = (f32[4,128]{1,0:T(4,128)S(1)}, f32[4,128]{1,0:T(4,128)S(1)}, u32[]{:S(2)}, u32[]{:S(2)}) collective-permute-start(f32[4,128]{1,0:T(4,128)S(1)} %shard_map.106), channel_id=1, source_target_pairs={{0,0},{1,32},{2,64},{3,96},{4,128},{5,160},{6,192},{7,224},{8,8},{... | collective-permute-start | bytes 6152 | tf_op jit(solution)/shard_map/ppermute | solution.py:55
  110.7 4.2 %shard_map.108.refs_8_ = f32[512,256]{1,0:T(8,128)S(1)} custom-call(s32[6]{0:T(128)S(1)} %stack.57.at_ref, f32[4,72,256]{2,1,0:T(8,128)S(1)} %all-to-all-done.2.own_ref, f32[4,72,256]{2,1,0:T(8,128)S(1)} %collective-permute-done.1.other_ref, f32[4,64,256]{2,1,0:T(8,128)S(1)} %pad_maximum_fusion.refs_0_, f32[4,64,256]{2,1,0:T(8,128)S(1)} %collective-permute-done.8.refs_1_, ...), custom_call_target="tpu_custom_call" | custom-call | flops 1610612736 | bytes 1048576 | tf_op jit(solution)/shard_map/pallas_call | solution.py:90
  114.9 2.7 %collective-permute-done.2 = f32[4,128]{1,0:T(4,128)S(1)} collective-permute-done((f32[4,128]{1,0:T(4,128)S(1)}, f32[4,128]{1,0:T(4,128)S(1)}, u32[]{:S(2)}, u32[]{:S(2)}) %collective-permute-start.2) | collective-permute-done | bytes 2080 | tf_op jit(solution)/shard_map/ppermute | solution.py:55
  118.2 3.3 %all-to-all-start.3 = ((f32[4,4,128]{2,1,0:T(4,128)}), f32[4,4,128]{2,1,0:T(4,128)S(1)}, u32[]{:S(2)}, u32[]{:S(2)}) async-start(f32[4,4,128]{2,1,0:T(4,128)} %broadcast_in_dim.14), calls=%async_computation.3 | async-start | bytes 16384 | tf_op jit(solution)/shard_map/all_to_all | solution.py:30
  123.4 4.2 %shard_map.109.screened_ref = f32[512,256]{1,0:T(8,128)S(1)} custom-call(s32[6]{0:T(128)S(1)} %stack.57.at_ref, f32[4,72,256]{2,1,0:T(8,128)S(1)} %all-to-all-done.2.own_ref, f32[4,72,256]{2,1,0:T(8,128)S(1)} %collective-permute-done.1.other_ref, f32[4,64,256]{2,1,0:T(8,128)S(1)} %pad_maximum_fusion.refs_0_, f32[4,64,256]{2,1,0:T(8,128)S(1)} %copy-done.1, ...), custom_call_target="tpu_custom_call" | custom-call | flops 1610612736 | bytes 1048576 | tf_op jit(solution)/shard_map/pallas_call | solution.py:90
  127.7 5.1 %shard_map.110 = (f32[16,8,8,128]{3,2,1,0:T(8,128)S(1)}, f32[16,8,8,128]{3,2,1,0:T(8,128)S(1)}) custom-call(s32[6]{0:T(128)S(1)} %stack.57.at_ref, f32[16,128]{1,0:T(8,128)S(1)} %bitcast.23, f32[512,256]{1,0:T(8,128)S(1)} %shard_map.109.screened_ref, f32[64,1280]{1,0:T(8,128)S(1)} %get-tuple-element.13.points_ref.refs_0_, ...), custom_call_target="tpu_custom_call" | custom-call | flops 536870912 | bytes 1048576 | tf_op jit(solution)/shard_map/pallas_call | solution.py:90
  132.8 1.9 %collective-permute-done.24 = f32[16,8,8,128]{3,2,1,0:T(8,128)S(1)} collective-permute-done((f32[16,8,8,128]{3,2,1,0:T(8,128)S(1)}, f32[16,8,8,128]{3,2,1,0:T(8,128)S(1)}, u32[]{:S(2)}, u32[]{:S(2)}) %collective-permute-start.24) | collective-permute-done | bytes 524320 | tf_op jit(solution)/shard_map/ppermute | solution.py:38
  134.8 18.4 %all_to_all.37.parts_ref = f32[16,8,8,128]{3,2,1,0:T(8,128)S(1)} all-to-all(f32[16,8,8,128]{3,2,1,0:T(8,128)S(1)} %add.7), channel_id=1, replica_groups=mesh['row_0'=4,'row_1'=2,'row_2'=4,'col_0'=4,'col_1'=2] {'row_0','row_2'}, dimensions={0} | all-to-all | bytes 1048576 | tf_op jit(solution)/shard_map/all_to_all | solution.py:30
  153.9 3.4 %all-to-all-start.5 = ((f32[8,8,8,128]{3,2,1,0:T(8,128)}), f32[8,8,8,128]{3,2,1,0:T(8,128)S(1)}, u32[]{:S(2)}, u32[]{:S(2)}) async-start(f32[8,8,8,128]{3,2,1,0:T(8,128)} %shard_map.111), calls=%async_computation.5 | async-start | bytes 524288 | tf_op jit(solution)/shard_map/all_to_all | solution.py:30
  158.0 8.5 %all-to-all-done.5.parts_ref = f32[8,8,8,128]{3,2,1,0:T(8,128)S(1)} async-done(((f32[8,8,8,128]{3,2,1,0:T(8,128)}), f32[8,8,8,128]{3,2,1,0:T(8,128)S(1)}, u32[]{:S(2)}, u32[]{:S(2)}) %all-to-all-start.5) | async-done | bytes 262176 | tf_op jit(solution)/shard_map/all_to_all | solution.py:30
  166.5 14.5 %all_to_all.38.sums_ref = f32[32,1,128]{2,1,0:T(1,128)S(1)} all-to-all(f32[32,1,128]{2,1,0:T(1,128)S(1)} %get-tuple-element.18), channel_id=1, replica_groups=mesh['row_0'=4,'row_1'=2,'row_2'=4,'col_0'=4,'col_1'=2] {'row_0','row_2'..., dimensions={0} | all-to-all | bytes 32768 | tf_op jit(solution)/shard_map/all_to_all | solution.py:30
  181.0 1.3 shard_map.113
  (61 shorter events, 12.3 us)
Async XLA Ops:
  35.7 20.4 %collective-permute-start = (f32[16,8,8,128]{3,2,1,0:T(8,128)S(1)}, f32[16,8,8,128]{3,2,1,0:T(8,128)S(1)}, u32[]{:S(2)}, u32[]{:S(2)}) collective-permute-start(f32[16,8,8,128]{3,2,1,0:T(8,128)S(1)} %all_to_all.36.own_ref), channel_id=1, source_target_pairs={{0,1},{1,0},{2,3},{3,2},{4,5},{5,4},{6,7},{7,6},{8,9},{9,8},{10,11... | collective-permute-start | bytes 1572872 | tf_op jit(solution)/shard_map/ppermute | solution.py:38
  39.0 10.6 %collective-permute-start.3 = (f32[64,256]{1,0:T(8,128)}, f32[64,256]{1,0:T(8,128)S(1)}, u32[]{:S(2)}, u32[]{:S(2)}) collective-permute-start(f32[64,256]{1,0:T(8,128)} %pv_hbm.1), channel_id=1, source_target_pairs={{0,0},{1,32},{2,64},{3,96},{4,128},{5,160},{6,192},{7,224},{8,8},{... | collective-permute-start | bytes 196616 | tf_op jit(solution)/shard_map/ppermute | solution.py:55
  41.2 8.3 %collective-permute-start.4 = (f32[64,256]{1,0:T(8,128)}, f32[64,256]{1,0:T(8,128)S(1)}, u32[]{:S(2)}, u32[]{:S(2)}) collective-permute-start(f32[64,256]{1,0:T(8,128)} %pv_hbm.1), channel_id=1, source_target_pairs={{0,32},{1,0},{2,96},{3,64},{4,160},{5,128},{6,224},{7,192},{8,40},... | collective-permute-start | bytes 196616 | tf_op jit(solution)/shard_map/ppermute | solution.py:55
  50.1 13.7 %collective-permute-start.5 = (f32[64,256]{1,0:T(8,128)S(1)}, f32[64,256]{1,0:T(8,128)S(1)}, u32[]{:S(2)}, u32[]{:S(2)}) collective-permute-start(f32[64,256]{1,0:T(8,128)S(1)} %get-tuple-element.14), channel_id=1, source_target_pairs={{8,0},{16,8},{24,16},{0,24},{9,1},{17,9},{25,17},{1,25},{10,2},{18... | collective-permute-start | bytes 196616 | tf_op jit(solution)/shard_map/ppermute | solution.py:42
  50.4 13.9 %collective-permute-start.6 = (f32[64,256]{1,0:T(8,128)S(1)}, f32[64,256]{1,0:T(8,128)S(1)}, u32[]{:S(2)}, u32[]{:S(2)}) collective-permute-start(f32[64,256]{1,0:T(8,128)S(1)} %get-tuple-element.14), channel_id=1, source_target_pairs={{16,0},{24,8},{0,16},{8,24},{17,1},{25,9},{1,17},{9,25},{18,2},{26... | collective-permute-start | bytes 196616 | tf_op jit(solution)/shard_map/ppermute | solution.py:42
  52.2 12.8 %collective-permute-start.7 = (f32[64,256]{1,0:T(8,128)S(1)}, f32[64,256]{1,0:T(8,128)S(1)}, u32[]{:S(2)}, u32[]{:S(2)}) collective-permute-start(f32[64,256]{1,0:T(8,128)S(1)} %get-tuple-element.14), channel_id=1, source_target_pairs={{24,0},{0,8},{8,16},{16,24},{25,1},{1,9},{9,17},{17,25},{26,2},{2,... | collective-permute-start | bytes 196616 | tf_op jit(solution)/shard_map/ppermute | solution.py:42
  52.2 20.5 %collective-permute-start.17 = (f32[64,1280]{1,0:T(8,128)S(1)}, f32[64,1280]{1,0:T(8,128)}, u32[]{:S(2)}, u32[]{:S(2)}) collective-permute-start(f32[64,1280]{1,0:T(8,128)S(1)} %get-tuple-element.13.points_ref.refs_0_), channel_id=1, source_target_pairs={{2,0},{4,2},{6,4},{0,6},{3,1},{5,3},{7,5},{1,7},{10,8},{12,10},{14... | collective-permute-start | bytes 983048 | tf_op jit(solution)/shard_map/ppermute | solution.py:42
  58.0 14.7 %all-to-all-start.2 = ((f32[4,72,256]{2,1,0:T(8,128)}), f32[4,72,256]{2,1,0:T(8,128)S(1)}, u32[]{:S(2)}, u32[]{:S(2)}) async-start(f32[4,72,256]{2,1,0:T(8,128)} %shard_map.105), calls=%async_computation.2 | async-start | bytes 589824 | tf_op jit(solution)/shard_map/all_to_all | solution.py:30
  61.5 30.4 %collective-permute-start.18 = (f32[64,1280]{1,0:T(8,128)S(1)}, f32[64,1280]{1,0:T(8,128)}, u32[]{:S(2)}, u32[]{:S(2)}) collective-permute-start(f32[64,1280]{1,0:T(8,128)S(1)} %get-tuple-element.13.points_ref.refs_0_), channel_id=1, source_target_pairs={{4,0},{6,2},{0,4},{2,6},{5,1},{7,3},{1,5},{3,7},{12,8},{14,10},{8,... | collective-permute-start | bytes 983048 | tf_op jit(solution)/shard_map/ppermute | solution.py:42
  63.8 3.4 %collective-permute-start.11 = (f32[64,256]{1,0:T(8,128)S(1)}, f32[64,256]{1,0:T(8,128)S(1)}, u32[]{:S(2)}, u32[]{:S(2)}) collective-permute-start(f32[64,256]{1,0:T(8,128)S(1)} %get-tuple-element.15), channel_id=1, source_target_pairs={{64,0},{128,64},{192,128},{0,192},{65,1},{129,65},{193,129},{1,193... | collective-permute-start | bytes 196616 | tf_op jit(solution)/shard_map/ppermute | solution.py:42
  64.3 4.6 %collective-permute-start.12 = (f32[64,256]{1,0:T(8,128)S(1)}, f32[64,256]{1,0:T(8,128)S(1)}, u32[]{:S(2)}, u32[]{:S(2)}) collective-permute-start(f32[64,256]{1,0:T(8,128)S(1)} %get-tuple-element.15), channel_id=1, source_target_pairs={{128,0},{192,64},{0,128},{64,192},{129,1},{193,65},{1,129},{65,193... | collective-permute-start | bytes 196616 | tf_op jit(solution)/shard_map/ppermute | solution.py:42
  65.0 4.9 %collective-permute-start.13 = (f32[64,256]{1,0:T(8,128)S(1)}, f32[64,256]{1,0:T(8,128)S(1)}, u32[]{:S(2)}, u32[]{:S(2)}) collective-permute-start(f32[64,256]{1,0:T(8,128)S(1)} %get-tuple-element.15), channel_id=1, source_target_pairs={{192,0},{0,64},{64,128},{128,192},{193,1},{1,65},{65,129},{129,193... | collective-permute-start | bytes 196616 | tf_op jit(solution)/shard_map/ppermute | solution.py:42
  67.2 27.6 %collective-permute-start.19 = (f32[64,1280]{1,0:T(8,128)S(1)}, f32[64,1280]{1,0:T(8,128)}, u32[]{:S(2)}, u32[]{:S(2)}) collective-permute-start(f32[64,1280]{1,0:T(8,128)S(1)} %get-tuple-element.13.points_ref.refs_0_), channel_id=1, source_target_pairs={{6,0},{0,2},{2,4},{4,6},{7,1},{1,3},{3,5},{5,7},{14,8},{8,10},{10,... | collective-permute-start | bytes 983048 | tf_op jit(solution)/shard_map/ppermute | solution.py:42
  68.9 26.1 %collective-permute-start.10 = (f32[4,64,256]{2,1,0:T(8,128)S(1)}, f32[4,64,256]{2,1,0:T(8,128)S(1)}, u32[]{:S(2)}, u32[]{:S(2)}) collective-permute-start(f32[4,64,256]{2,1,0:T(8,128)S(1)} %pad_maximum_fusion.refs_0_), channel_id=1, source_target_pairs={{192,0},{0,64},{64,128},{128,192},{193,1},{1,65},{65,129},{129,193... | collective-permute-start | bytes 786440 | tf_op jit(solution)/shard_map/ppermute | solution.py:42
  69.9 25.6 %collective-permute-start.14 = (f32[4,64,256]{2,1,0:T(8,128)S(1)}, f32[4,64,256]{2,1,0:T(8,128)S(1)}, u32[]{:S(2)}, u32[]{:S(2)}) collective-permute-start(f32[4,64,256]{2,1,0:T(8,128)S(1)} %pad_maximum_fusion.1.refs_4_), channel_id=1, source_target_pairs={{8,0},{16,8},{24,16},{0,24},{9,1},{17,9},{25,17},{1,25},{10,2},{18... | collective-permute-start | bytes 786440 | tf_op jit(solution)/shard_map/ppermute | solution.py:42
  72.7 35.1 %collective-permute-start.1 = (f32[4,72,256]{2,1,0:T(8,128)S(1)}, f32[4,72,256]{2,1,0:T(8,128)S(1)}, u32[]{:S(2)}, u32[]{:S(2)}) collective-permute-start(f32[4,72,256]{2,1,0:T(8,128)S(1)} %all-to-all-done.2.own_ref), channel_id=1, source_target_pairs={{0,1},{1,0},{2,3},{3,2},{4,5},{5,4},{6,7},{7,6},{8,9},{9,8},{10,11... | collective-permute-start | bytes 884744 | tf_op jit(solution)/shard_map/ppermute | solution.py:38
  91.8 8.1 %collective-permute-start.15 = (f32[4,64,256]{2,1,0:T(8,128)S(1)}, f32[4,64,256]{2,1,0:T(8,128)S(1)}, u32[]{:S(2)}, u32[]{:S(2)}) collective-permute-start(f32[4,64,256]{2,1,0:T(8,128)S(1)} %pad_maximum_fusion.1.refs_4_), channel_id=1, source_target_pairs={{16,0},{24,8},{0,16},{8,24},{17,1},{25,9},{1,17},{9,25},{18,2},{26... | collective-permute-start | bytes 786440 | tf_op jit(solution)/shard_map/ppermute | solution.py:42
  94.8 12.1 %collective-permute-start.16 = (f32[4,64,256]{2,1,0:T(8,128)S(1)}, f32[4,64,256]{2,1,0:T(8,128)S(1)}, u32[]{:S(2)}, u32[]{:S(2)}) collective-permute-start(f32[4,64,256]{2,1,0:T(8,128)S(1)} %pad_maximum_fusion.1.refs_4_), channel_id=1, source_target_pairs={{24,0},{0,8},{8,16},{16,24},{25,1},{1,9},{9,17},{17,25},{26,2},{2,... | collective-permute-start | bytes 786440 | tf_op jit(solution)/shard_map/ppermute | solution.py:42
  95.0 12.6 %collective-permute-start.8 = (f32[4,64,256]{2,1,0:T(8,128)S(1)}, f32[4,64,256]{2,1,0:T(8,128)S(1)}, u32[]{:S(2)}, u32[]{:S(2)}) collective-permute-start(f32[4,64,256]{2,1,0:T(8,128)S(1)} %pad_maximum_fusion.refs_0_), channel_id=1, source_target_pairs={{64,0},{128,64},{192,128},{0,192},{65,1},{129,65},{193,129},{1,193... | collective-permute-start | bytes 786440 | tf_op jit(solution)/shard_map/ppermute | solution.py:42
  95.5 13.3 %collective-permute-start.9 = (f32[4,64,256]{2,1,0:T(8,128)S(1)}, f32[4,64,256]{2,1,0:T(8,128)S(1)}, u32[]{:S(2)}, u32[]{:S(2)}) collective-permute-start(f32[4,64,256]{2,1,0:T(8,128)S(1)} %pad_maximum_fusion.refs_0_), channel_id=1, source_target_pairs={{128,0},{192,64},{0,128},{64,192},{129,1},{193,65},{1,129},{65,193... | collective-permute-start | bytes 786440 | tf_op jit(solution)/shard_map/ppermute | solution.py:42
  99.9 27.7 %collective-permute-start.20 = (f32[64,1280]{1,0:T(8,128)S(1)}, f32[64,1280]{1,0:T(8,128)}, u32[]{:S(2)}, u32[]{:S(2)}) collective-permute-start(f32[64,1280]{1,0:T(8,128)S(1)} %get-tuple-element.13.points_ref.refs_0_), channel_id=1, source_target_pairs={{0,1},{1,0},{2,3},{3,2},{4,5},{5,4},{6,7},{7,6},{8,9},{9,8},{10,11... | collective-permute-start | bytes 983048 | tf_op jit(solution)/shard_map/ppermute | solution.py:38
  106.8 20.8 %collective-permute-start.21 = (f32[64,1280]{1,0:T(8,128)}, f32[64,1280]{1,0:T(8,128)}, u32[]{:S(2)}, u32[]{:S(2)}) collective-permute-start(f32[64,1280]{1,0:T(8,128)} %collective-permute-done.17.refs_1_), channel_id=1, source_target_pairs={{0,1},{1,0},{2,3},{3,2},{4,5},{5,4},{6,7},{7,6},{8,9},{9,8},{10,11... | collective-permute-start | bytes 983048 | tf_op jit(solution)/shard_map/ppermute | solution.py:38
  107.7 10.5 %copy-start = (f32[4,64,256]{2,1,0:T(8,128)}, f32[4,64,256]{2,1,0:T(8,128)S(1)}, u32[]{:S(2)}) copy-start(f32[4,64,256]{2,1,0:T(8,128)S(1)} %collective-permute-done.8.refs_1_) | copy-start | bytes 786436
  107.7 19.9 %collective-permute-start.22 = (f32[64,1280]{1,0:T(8,128)}, f32[64,1280]{1,0:T(8,128)}, u32[]{:S(2)}, u32[]{:S(2)}) collective-permute-start(f32[64,1280]{1,0:T(8,128)} %collective-permute-done.18.refs_2_), channel_id=1, source_target_pairs={{0,1},{1,0},{2,3},{3,2},{4,5},{5,4},{6,7},{7,6},{8,9},{9,8},{10,11... | collective-permute-start | bytes 983048 | tf_op jit(solution)/shard_map/ppermute | solution.py:38
  107.8 19.8 %collective-permute-start.23 = (f32[64,1280]{1,0:T(8,128)}, f32[64,1280]{1,0:T(8,128)}, u32[]{:S(2)}, u32[]{:S(2)}) collective-permute-start(f32[64,1280]{1,0:T(8,128)} %collective-permute-done.19.refs_3_), channel_id=1, source_target_pairs={{0,1},{1,0},{2,3},{3,2},{4,5},{5,4},{6,7},{7,6},{8,9},{9,8},{10,11... | collective-permute-start | bytes 983048 | tf_op jit(solution)/shard_map/ppermute | solution.py:38
  108.8 9.4 %copy-start.2 = (f32[4,64,256]{2,1,0:T(8,128)}, f32[4,64,256]{2,1,0:T(8,128)S(1)}, u32[]{:S(2)}) copy-start(f32[4,64,256]{2,1,0:T(8,128)S(1)} %collective-permute-done.9.refs_2_) | copy-start | bytes 786436
  108.8 8.8 %collective-permute-start.2 = (f32[4,128]{1,0:T(4,128)S(1)}, f32[4,128]{1,0:T(4,128)S(1)}, u32[]{:S(2)}, u32[]{:S(2)}) collective-permute-start(f32[4,128]{1,0:T(4,128)S(1)} %shard_map.106), channel_id=1, source_target_pairs={{0,0},{1,32},{2,64},{3,96},{4,128},{5,160},{6,192},{7,224},{8,8},{... | collective-permute-start | bytes 6152 | tf_op jit(solution)/shard_map/ppermute | solution.py:55
  118.2 9.4 %all-to-all-start.3 = ((f32[4,4,128]{2,1,0:T(4,128)}), f32[4,4,128]{2,1,0:T(4,128)S(1)}, u32[]{:S(2)}, u32[]{:S(2)}) async-start(f32[4,4,128]{2,1,0:T(4,128)} %broadcast_in_dim.14), calls=%async_computation.3 | async-start | bytes 16384 | tf_op jit(solution)/shard_map/all_to_all | solution.py:30
  127.6 38.8 %copy-start.5 = (f32[8,3,8,128]{3,2,1,0:T(8,128)S(1)}, f32[8,3,8,128]{3,2,1,0:T(8,128)}, u32[]{:S(2)}) copy-start(f32[8,3,8,128]{3,2,1,0:T(8,128)} %copy-done.4) | copy-start | bytes 294916
  127.6 53.4 %copy-start.6 = (f32[1,8,128]{2,1,0:T(8,128)S(1)}, f32[1,8,128]{2,1,0:T(8,128)}, u32[]{:S(2)}) copy-start(f32[1,8,128]{2,1,0:T(8,128)} %param.9) | copy-start | bytes 12292
  132.7 2.0 %collective-permute-start.24 = (f32[16,8,8,128]{3,2,1,0:T(8,128)S(1)}, f32[16,8,8,128]{3,2,1,0:T(8,128)S(1)}, u32[]{:S(2)}, u32[]{:S(2)}) collective-permute-start(f32[16,8,8,128]{3,2,1,0:T(8,128)S(1)} %get-tuple-element.17), channel_id=1, source_target_pairs={{0,1},{1,0},{2,3},{3,2},{4,5},{5,4},{6,7},{7,6},{8,9},{9,8},{10,11... | collective-permute-start | bytes 1572872 | tf_op jit(solution)/shard_map/ppermute | solution.py:38
  153.9 12.5 %all-to-all-start.5 = ((f32[8,8,8,128]{3,2,1,0:T(8,128)}), f32[8,8,8,128]{3,2,1,0:T(8,128)S(1)}, u32[]{:S(2)}, u32[]{:S(2)}) async-start(f32[8,8,8,128]{3,2,1,0:T(8,128)} %shard_map.111), calls=%async_computation.5 | async-start | bytes 524288 | tf_op jit(solution)/shard_map/all_to_all | solution.py:30
  (4 other events, 3.2 us)

commit v2 on v1

--- a/solution.py
+++ b/solution.py
@@ -174,50 +174,35 @@
         out_ref[l : l + 1, :] = first + pltpu.roll(second, 64, 1)
 
 
-def screened_kernel(turns, at_ref, own_ref, other_ref, *refs):
-    a_refs, b_refs, refs = refs[:4], refs[4:8], refs[8:]
-    so_far_ref = None
-    if turns[0] > 0:
-        so_far_ref, refs = refs[0], refs[1:]
-    core, x, y = at_ref[0], at_ref[1], at_ref[2]
-    w_hbm, out_ref, w_ref, terms_ref, sems = refs
+def screened_kernel(side, at_ref, rows_ref, *refs):
+    a_refs, b_refs, (w_hbm, out_ref, w_ref, terms_ref, sems) = refs[:4], refs[4:8], refs[8:]
+    which = at_ref[0] if side == 0 else 1 - at_ref[0]
+    x, y = at_ref[1], at_ref[2]
     moves = []
-    for n, t in enumerate(turns):
-        for s in range(4):
-            at = pl.multiple_of(lax.rem(y + s, 4) * 512 + lax.rem(x + t, 4) * 128, 128)
-            moves.append(
-                pltpu.make_async_copy(
-                    w_hbm.at[:, pl.ds(at, 128)], w_ref.at[n * 4 + s], sems.at[n * 4 + s]
-                )
-            )
-            moves[-1].start()
-    pairs = [
-        halves(jnp.concatenate([r[l, :64] for l in range(4)], axis=0)) for r in (own_ref, other_ref)
-    ]
-    for n, t in enumerate(turns):
+    for l in range(4):
+        rows = pl.ds(pl.multiple_of((2 * l + which) * 64, 64), 64)
+        moves.append(pltpu.make_async_copy(w_hbm.at[rows, :], w_ref.at[l], sems.at[l]))
+        moves[-1].start()
+    pair = halves(jnp.concatenate([rows_ref[l, :64] for l in range(4)], axis=0))
+    for t in range(4):
         points = [piece for s in range(4) for piece in (a_refs[t][s], b_refs[s][t])]
         points = halves(jnp.concatenate(points, axis=0))
-        for side, which in enumerate((core, 1 - core)):
-            terms_ref[...] = product(pairs[side], points, ROWS_BY_ROWS)
+        terms_ref[...] = product(pair, points, ROWS_BY_ROWS)
+        for l in range(4):
+            if t == 0:
+                moves[l].wait()
             for s in range(4):
-                if side == 0:
-                    moves[n * 4 + s].wait()
-                for l in range(4):
-                    rows = pl.ds(pl.multiple_of((2 * l + which) * 64, 64), 64)
-                    here = (slice(l * 64, l * 64 + 64), slice(s * 128, s * 128 + 128))
-                    terms_ref[here] = terms_ref[here] * w_ref[n * 4 + s, rows, :]
-            done = product(halves(terms_ref[...]), points, PLAIN)
-            mine = slice(side * 256, side * 256 + 256)
-            if n > 0:
-                done += out_ref[mine]
-            elif so_far_ref is not None:
-                done += so_far_ref[mine]
-            out_ref[mine] = done
-
-
-def contribution_kernel(at_ref, density_ref, screened_ref, *refs):
-    points_refs, (b_hbm, own_ref, other_ref, b_ref, sems) = refs[:8], refs[8:]
-    core, z = at_ref[0], at_ref[4]
+                at = pl.multiple_of(lax.rem(y + s, 4) * 512 + lax.rem(x + t, 4) * 128, 128)
+                here = (slice(l * 64, l * 64 + 64), slice(s * 128, s * 128 + 128))
+                terms_ref[here] = terms_ref[here] * w_ref[l, :, pl.ds(at, 128)]
+        done = product(halves(terms_ref[...]), points, PLAIN)
+        out_ref[...] = done if t == 0 else out_ref[...] + done
+
+
+def contribution_kernel(at_ref, *refs):
+    density_refs, screened_refs, points_refs = refs[:4], refs[4:6], refs[6:14]
+    b_hbm, own_ref, other_ref, b_ref, density_ref, sems = refs[14:]
+    core, y, z = at_ref[0], at_ref[2], at_ref[4]
     moves = []
     for side, which in enumerate((core, 1 - core)):
         for s in range(4):
@@ -227,6 +212,12 @@
                 pltpu.make_async_copy(b_hbm.at[pl.ds(at, 64), :], b_ref.at[n], sems.at[n])
             )
             moves[-1].start()
+    for s in range(4):
+        density_ref[lax.rem(y + s, 4)] = density_refs[s][...]
+    columns = [
+        halves(jnp.concatenate([columns_of(r, which) for r in points_refs], axis=0))
+        for which in (1 - core, core)
+    ]
     source = []
     for side in range(2):
         for s in range(4):
@@ -235,14 +226,13 @@
             moves[side * 4 + s].wait()
             for n in range(16):
                 tile = b_ref[side * 4 + s, :, n * 128 : n * 128 + 128]
-                total += tile * density_ref[n : n + 1, :]
+                total += tile * density_ref[n // 4, n % 4 : n % 4 + 1, :]
             potential = jnp.sum(total, axis=1, keepdims=True)
-            screened = screened_ref[pl.ds(pl.multiple_of(side * 256 + l * 64, 64), 64), :]
+            screened = screened_refs[side][pl.ds(pl.multiple_of(l * 64, 64), 64), :]
             source.append(2.0 * potential * points_refs[side * 4 + s][:, :V] - screened)
     source = halves(jnp.concatenate(source, axis=0))
-    for ref, which in ((other_ref, 1 - core), (own_ref, core)):
-        columns = halves(jnp.concatenate([columns_of(r, which) for r in points_refs], axis=0))
-        done = product(source, columns, COLUMNS_BY_COLUMNS)
+    for ref, part in zip((other_ref, own_ref), columns):
+        done = product(source, part, COLUMNS_BY_COLUMNS)
         for x in range(4):
             for h in range(2):
                 for y in range(4):
@@ -331,25 +321,24 @@
     other_rows = from_partner(own_rows)
     row_density = local_kernel(density_kernel, [(4, 128)], 1 << 10)(at, own_rows, other_rows)
     swapped = grid_swap(row_density, 0)
-    far_density = from_all(swapped, Y).reshape(16, 128)
-
-    screened = ()
-    for turns in ((0, 1), (2, 3)):
-        scratch = [pltpu.VMEM((8, 512, 128), f32), pltpu.VMEM((256, 512), f32)]
-        scratch.append(pltpu.SemaphoreType.DMA((8,)))
-        kernel = functools.partial(screened_kernel, turns)
-        done = local_kernel(kernel, [(512, V)], 3 << 29, scratch, 16)(
-            at, own_rows, other_rows, *a_parts, *b_parts, *screened, far=(screened_coulomb,)
+    far_density = [swapped] + [from_next(swapped, Y, s) for s in (1, 2, 3)]
+
+    screened = []
+    for side, there in enumerate((own_rows, other_rows)):
+        scratch = [pltpu.VMEM((4, 64, 2048), f32), pltpu.VMEM((256, 512), f32)]
+        scratch.append(pltpu.SemaphoreType.DMA((4,)))
+        kernel = functools.partial(screened_kernel, side)
+        screened.append(
+            local_kernel(kernel, [(256, V)], 3 << 29, scratch, 16)(
+                at, there, *a_parts, *b_parts, far=(screened_coulomb,)
+            )
         )
-        screened = (done,)
-
+
+    scratch = [pltpu.VMEM((8, 64, 2048), f32), pltpu.VMEM((4, 4, 128), f32)]
+    scratch.append(pltpu.SemaphoreType.DMA((8,)))
     own_half, other_half = local_kernel(
-        contribution_kernel,
-        [(16, 8, 8, 128)] * 2,
-        1 << 29,
-        [pltpu.VMEM((8, 64, 2048), f32), pltpu.SemaphoreType.DMA((8,))],
-        16,
-    )(at, far_density, *screened, *rows, far=(bare_coulomb,))
+        contribution_kernel, [(16, 8, 8, 128)] * 2, 1 << 29, scratch, 16
+    )(at, *far_density, *screened, *rows, far=(bare_coulomb,))
     own_half += from_partner(other_half)
     parts = copies_to_all(own_half, (X, Y))
     copies = local_kernel(plane_sum_kernel, [(8, 8, 8, 128)], 1 << 18)(parts)

time: 183 us -> 174 us (0.951)
  starting transfers between devices: 56.3 us -> 42 us
  waiting for transfers between devices: 35.3 us -> 45.6 us
  local copies, waits for them, and re-layouts: 3.87 us -> 0.79 us
    ppermute x7, starting transfers between devices: 22.8 us -> 9.9 us  [from_partner(): return lax.ppermute(block, K, [(0, 1), (1, 0)])]
    ppermute x15 -> x18, waiting for transfers between devices: 14.1 us -> 22.6 us  [from_next(): return lax.ppermute(block, axis, [((i + shift) % 4, i) for i in range(4)])]
    all_to_all x3 -> x2, waiting for transfers between devices: 8.47 us -> 11.2 us  [copies_to_all(): return lax.all_to_all(copies, axes, split_axis=0, concat_axis=0, tiled=True)]
    unnamed x16 -> x4, local copies, waits for them, and re-layouts: 3.14 us -> 0.65 us
    all_to_all x3 -> x2, starting transfers between devices: 10.1 us -> 7.84 us  [copies_to_all(): return lax.all_to_all(copies, axes, split_axis=0, concat_axis=0, tiled=True)]
    ppermute x15 -> x18, starting transfers between devices: 19 us -> 19.2 us  [from_next(): return lax.ppermute(block, axis, [((i + shift) % 4, i) for i in range(4)])]
  transfers between devices with their start and end apart: 28 -> 30, of which waited for: 9 -> 11; matrix products, arithmetic and copies ran while one was open for 0% -> 0% of each run, Pallas kernels for 6% -> 7%
where the time goes in v2:
time: 174 us; the launch traced here: 173 us
  blocking collectives  64.1 us (37%)
  waiting for transfers between devices  45.6 us (26%)
  starting transfers between devices  42 us (24%)
  Pallas kernels  19.3 us (11%)
    all_to_all x4, blocking collectives, copies_to_all(): return lax.all_to_all(copies, axes, split_axis=0, concat_axis=0, tiled=True)  64.1 us
    ppermute x18, waiting for transfers between devices, from_next(): return lax.ppermute(block, axis, [((i + shift) % 4, i) for i in range(4)])  22.6 us
    pallas_call x10, Pallas kernels, call(): pl.pallas_call(body, out_shape=shapes if many else shapes[0], in_specs=sp...  19.3 us
    ppermute x18, starting transfers between devices, from_next(): return lax.ppermute(block, axis, [((i + shift) % 4, i) for i in range(4)])  19.2 us
    all_to_all x2, waiting for transfers between devices, copies_to_all(): return lax.all_to_all(copies, axes, split_axis=0, concat_axis=0, tiled=True)  11.2 us
    ppermute x3, waiting for transfers between devices, grid_swap(): return lax.ppermute(block, AXES, pairs)  9.96 us
    ppermute x7, starting transfers between devices, from_partner(): return lax.ppermute(block, K, [(0, 1), (1, 0)])  9.9 us
    all_to_all x2, starting transfers between devices, copies_to_all(): return lax.all_to_all(copies, axes, split_axis=0, concat_axis=0, tiled=True)  7.84 us
  transfers between devices with their start and end apart: 30, of which 11 were waited for; matrix products, arithmetic and copies ran while one was open for 0% of the time, Pallas kernels for 7%

profile of v2, /device:TPU:1, one launch (start us, length us, event | category | flops | bytes accessed | tf_op | source)
XLA Modules:
  0.0 173.4 jit_solution(1020327766456635173)
XLA Ops:
  1.3 1.6 shard_map.104
  2.9 16.4 %all_to_all.30.piece_ref = f32[8,3,8,128]{3,2,1,0:T(8,128)S(1)} all-to-all(f32[8,3,8,128]{3,2,1,0:T(8,128)S(1)} %get-tuple-element.12), channel_id=1, replica_groups=mesh['row_0'=4,'row_1'=2,'row_2'=4,'col_0'=4,'col_1'=2] {'row_1','col_0'}, dimensions={0} | all-to-all | bytes 196608 | tf_op jit(solution)/shard_map/all_to_all | solution.py:30
  19.4 15.8 %all_to_all.31.own_ref = f32[16,8,8,128]{3,2,1,0:T(8,128)S(1)} all-to-all(f32[16,8,8,128]{3,2,1,0:T(8,128)S(1)} %broadcast_in_dim.10), channel_id=1, replica_groups=mesh['row_0'=4,'row_1'=2,'row_2'=4,'col_0'=4,'col_1'=2] {'row_0','row_2'}, dimensions={0} | all-to-all | bytes 1048576 | tf_op jit(solution)/shard_map/all_to_all | solution.py:30
  35.1 3.2 %collective-permute-start = (f32[16,8,8,128]{3,2,1,0:T(8,128)S(1)}, f32[16,8,8,128]{3,2,1,0:T(8,128)S(1)}, u32[]{:S(2)}, u32[]{:S(2)}) collective-permute-start(f32[16,8,8,128]{3,2,1,0:T(8,128)S(1)} %all_to_all.31.own_ref), channel_id=1, source_target_pairs={{0,1},{1,0},{2,3},{3,2},{4,5},{5,4},{6,7},{7,6},{8,9},{9,8},{10,11... | collective-permute-start | bytes 1572872 | tf_op jit(solution)/shard_map/ppermute | solution.py:38
  38.4 2.3 %collective-permute-start.6 = (f32[64,256]{1,0:T(8,128)}, f32[64,256]{1,0:T(8,128)S(1)}, u32[]{:S(2)}, u32[]{:S(2)}) collective-permute-start(f32[64,256]{1,0:T(8,128)} %pv_hbm.1), channel_id=1, source_target_pairs={{0,0},{1,32},{2,64},{3,96},{4,128},{5,160},{6,192},{7,224},{8,8},{... | collective-permute-start | bytes 196616 | tf_op jit(solution)/shard_map/ppermute | solution.py:55
  40.9 8.1 %collective-permute-done.6.first_ref = f32[64,256]{1,0:T(8,128)S(1)} collective-permute-done((f32[64,256]{1,0:T(8,128)}, f32[64,256]{1,0:T(8,128)S(1)}, u32[]{:S(2)}, u32[]{:S(2)}) %collective-permute-start.6) | collective-permute-done | bytes 65568 | tf_op jit(solution)/shard_map/ppermute | solution.py:55
  49.8 3.8 %collective-permute-start.20 = (f32[64,1280]{1,0:T(8,128)S(1)}, f32[64,1280]{1,0:T(8,128)S(1)}, u32[]{:S(2)}, u32[]{:S(2)}) collective-permute-start(f32[64,1280]{1,0:T(8,128)S(1)} %get-tuple-element.13.points_ref.refs_6_), channel_id=1, source_target_pairs={{2,0},{4,2},{6,4},{0,6},{3,1},{5,3},{7,5},{1,7},{10,8},{12,10},{14... | collective-permute-start | bytes 983048 | tf_op jit(solution)/shard_map/ppermute | solution.py:42
  53.6 2.0 %shard_map.105 = f32[4,72,256]{2,1,0:T(8,128)} custom-call(s32[6]{0:T(128)S(1)} %stack.57.at_ref, f32[16,8,8,128]{3,2,1,0:T(8,128)S(1)} %all_to_all.31.own_ref, f32[16,8,8,128]{3,2,1,0:T(8,128)S(1)} %collective-permute-done.other_ref, f32[64,1280]{1,0:T(8,128)S(1)} %get-tuple-element.13.points_ref.refs_6_), custom_call_target="tpu_custom_call" | custom-call | flops 134217728 | bytes 1048576 | tf_op jit(solution)/shard_map/pallas_call | solution.py:90
  55.6 3.6 %all-to-all-start.2 = ((f32[4,72,256]{2,1,0:T(8,128)}), f32[4,72,256]{2,1,0:T(8,128)S(1)}, u32[]{:S(2)}, u32[]{:S(2)}) async-start(f32[4,72,256]{2,1,0:T(8,128)} %shard_map.105), calls=%async_computation.2 | async-start | bytes 589824 | tf_op jit(solution)/shard_map/all_to_all | solution.py:30
  59.2 1.9 %collective-permute-start.9 = (f32[64,256]{1,0:T(8,128)S(1)}, f32[64,256]{1,0:T(8,128)S(1)}, u32[]{:S(2)}, u32[]{:S(2)}) collective-permute-start(f32[64,256]{1,0:T(8,128)S(1)} %get-tuple-element.14), channel_id=1, source_target_pairs={{16,0},{24,8},{0,16},{8,24},{17,1},{25,9},{1,17},{9,25},{18,2},{26... | collective-permute-start | bytes 196616 | tf_op jit(solution)/shard_map/ppermute | solution.py:42
  61.1 1.6 collective-permute-start.14
  63.8 1.5 collective-permute-start.22
  65.8 1.9 %collective-permute-start.15 = (f32[64,256]{1,0:T(8,128)S(1)}, f32[64,256]{1,0:T(8,128)S(1)}, u32[]{:S(2)}, u32[]{:S(2)}) collective-permute-start(f32[64,256]{1,0:T(8,128)S(1)} %get-tuple-element.15), channel_id=1, source_target_pairs={{128,0},{192,64},{0,128},{64,192},{129,1},{193,65},{1,129},{65,193... | collective-permute-start | bytes 196616 | tf_op jit(solution)/shard_map/ppermute | solution.py:42
  68.2 2.2 %collective-permute-done.15 = f32[64,256]{1,0:T(8,128)S(1)} collective-permute-done((f32[64,256]{1,0:T(8,128)S(1)}, f32[64,256]{1,0:T(8,128)S(1)}, u32[]{:S(2)}, u32[]{:S(2)}) %collective-permute-start.15) | collective-permute-done | bytes 65568 | tf_op jit(solution)/shard_map/ppermute | solution.py:42
  70.4 1.9 %collective-permute-start.11 = (f32[4,64,256]{2,1,0:T(8,128)S(1)}, f32[4,64,256]{2,1,0:T(8,128)S(1)}, u32[]{:S(2)}, u32[]{:S(2)}) collective-permute-start(f32[4,64,256]{2,1,0:T(8,128)S(1)} %pad_maximum_fusion.refs_0_), channel_id=1, source_target_pairs={{64,0},{128,64},{192,128},{0,192},{65,1},{129,65},{193,129},{1,193... | collective-permute-start | bytes 786440 | tf_op jit(solution)/shard_map/ppermute | solution.py:42
  73.6 10.8 %collective-permute-done.21.refs_8_ = f32[64,1280]{1,0:T(8,128)S(1)} collective-permute-done((f32[64,1280]{1,0:T(8,128)S(1)}, f32[64,1280]{1,0:T(8,128)S(1)}, u32[]{:S(2)}, u32[]{:S(2)}) %collective-permute-start.21) | collective-permute-done | bytes 327712 | tf_op jit(solution)/shard_map/ppermute | solution.py:42
  85.2 2.4 %all-to-all-done.2.own_ref.rows_ref = f32[4,72,256]{2,1,0:T(8,128)S(1)} async-done(((f32[4,72,256]{2,1,0:T(8,128)}), f32[4,72,256]{2,1,0:T(8,128)S(1)}, u32[]{:S(2)}, u32[]{:S(2)}) %all-to-all-start.2) | async-done | bytes 294944 | tf_op jit(solution)/shard_map/all_to_all | solution.py:30
  88.9 1.6 collective-permute-start.18
  90.9 3.5 %collective-permute-start.24 = (f32[64,1280]{1,0:T(8,128)S(1)}, f32[64,1280]{1,0:T(8,128)S(1)}, u32[]{:S(2)}, u32[]{:S(2)}) collective-permute-start(f32[64,1280]{1,0:T(8,128)S(1)} %collective-permute-done.20.refs_7_), channel_id=1, source_target_pairs={{0,1},{1,0},{2,3},{3,2},{4,5},{5,4},{6,7},{7,6},{8,9},{9,8},{10,11... | collective-permute-start | bytes 983048 | tf_op jit(solution)/shard_map/ppermute | solution.py:38
  94.4 4.0 %collective-permute-done.18.refs_6_ = f32[4,64,256]{2,1,0:T(8,128)S(1)} collective-permute-done((f32[4,64,256]{2,1,0:T(8,128)S(1)}, f32[4,64,256]{2,1,0:T(8,128)S(1)}, u32[]{:S(2)}, u32[]{:S(2)}) %collective-permute-start.18) | collective-permute-done | bytes 262176 | tf_op jit(solution)/shard_map/ppermute | solution.py:42
  100.3 4.0 %collective-permute-done.19.refs_7_ = f32[4,64,256]{2,1,0:T(8,128)S(1)} collective-permute-done((f32[4,64,256]{2,1,0:T(8,128)S(1)}, f32[4,64,256]{2,1,0:T(8,128)S(1)}, u32[]{:S(2)}, u32[]{:S(2)}) %collective-permute-start.19) | collective-permute-done | bytes 262176 | tf_op jit(solution)/shard_map/ppermute | solution.py:42
  104.3 2.7 %collective-permute-start.2 = (f32[4,128]{1,0:T(4,128)S(1)}, f32[4,128]{1,0:T(4,128)S(1)}, u32[]{:S(2)}, u32[]{:S(2)}) collective-permute-start(f32[4,128]{1,0:T(4,128)S(1)} %shard_map.106), channel_id=1, source_target_pairs={{0,0},{1,32},{2,64},{3,96},{4,128},{5,160},{6,192},{7,224},{8,8},{... | collective-permute-start | bytes 6152 | tf_op jit(solution)/shard_map/ppermute | solution.py:55
  107.1 4.2 %shard_map.108.refs_4_ = f32[256,256]{1,0:T(8,128)S(1)} custom-call(s32[6]{0:T(128)S(1)} %stack.57.at_ref, f32[4,72,256]{2,1,0:T(8,128)S(1)} %all-to-all-done.2.own_ref.rows_ref, f32[4,64,256]{2,1,0:T(8,128)S(1)} %pad_maximum_fusion.refs_0_, f32[4,64,256]{2,1,0:T(8,128)S(1)} %collective-permute-done.11.refs_1_, ...), custom_call_target="tpu_custom_call" | custom-call | flops 1610612736 | bytes 1048576 | tf_op jit(solution)/shard_map/pallas_call | solution.py:90
  111.2 1.9 %collective-permute-done.2.refs_0_ = f32[4,128]{1,0:T(4,128)S(1)} collective-permute-done((f32[4,128]{1,0:T(4,128)S(1)}, f32[4,128]{1,0:T(4,128)S(1)}, u32[]{:S(2)}, u32[]{:S(2)}) %collective-permute-start.2) | collective-permute-done | bytes 2080 | tf_op jit(solution)/shard_map/ppermute | solution.py:55
  113.1 1.5 collective-permute-start.4
  115.3 4.2 %shard_map.109.refs_5_ = f32[256,256]{1,0:T(8,128)S(1)} custom-call(s32[6]{0:T(128)S(1)} %stack.57.at_ref, f32[4,72,256]{2,1,0:T(8,128)S(1)} %collective-permute-done.1.other_ref.rows_ref, f32[4,64,256]{2,1,0:T(8,128)S(1)} %pad_maximum_fusion.refs_0_, f32[4,64,256]{2,1,0:T(8,128)S(1)} %collective-permute-done.11.refs_1_, ...), custom_call_target="tpu_custom_call" | custom-call | flops 1610612736 | bytes 1048576 | tf_op jit(solution)/shard_map/pallas_call | solution.py:90
  119.6 4.0 %shard_map.110 = (f32[16,8,8,128]{3,2,1,0:T(8,128)S(1)}, f32[16,8,8,128]{3,2,1,0:T(8,128)S(1)}) custom-call(s32[6]{0:T(128)S(1)} %stack.57.at_ref, f32[4,128]{1,0:T(4,128)S(1)} %collective-permute-done.2.refs_0_, f32[4,128]{1,0:T(4,128)S(1)} %collective-permute-done.3.refs_1_, f32[4,128]{1,0:T(4,128)S(1)} %collective-permute-done.4.refs_2_, ...), custom_call_target="tpu_custom_call" | custom-call | flops 536870912 | bytes 1048576 | tf_op jit(solution)/shard_map/pallas_call | solution.py:90
  123.7 1.9 %collective-permute-done.27 = f32[16,8,8,128]{3,2,1,0:T(8,128)S(1)} collective-permute-done((f32[16,8,8,128]{3,2,1,0:T(8,128)S(1)}, f32[16,8,8,128]{3,2,1,0:T(8,128)S(1)}, u32[]{:S(2)}, u32[]{:S(2)}) %collective-permute-start.27) | collective-permute-done | bytes 524320 | tf_op jit(solution)/shard_map/ppermute | solution.py:38
  125.7 17.7 %all_to_all.32.parts_ref = f32[16,8,8,128]{3,2,1,0:T(8,128)S(1)} all-to-all(f32[16,8,8,128]{3,2,1,0:T(8,128)S(1)} %add.7), channel_id=1, replica_groups=mesh['row_0'=4,'row_1'=2,'row_2'=4,'col_0'=4,'col_1'=2] {'row_0','row_2'}, dimensions={0} | all-to-all | bytes 1048576 | tf_op jit(solution)/shard_map/all_to_all | solution.py:30
  144.1 4.2 %all-to-all-start.4 = ((f32[8,8,8,128]{3,2,1,0:T(8,128)}), f32[8,8,8,128]{3,2,1,0:T(8,128)S(1)}, u32[]{:S(2)}, u32[]{:S(2)}) async-start(f32[8,8,8,128]{3,2,1,0:T(8,128)} %shard_map.111), calls=%async_computation.4 | async-start | bytes 524288 | tf_op jit(solution)/shard_map/all_to_all | solution.py:30
  149.0 8.8 %all-to-all-done.4.parts_ref = f32[8,8,8,128]{3,2,1,0:T(8,128)S(1)} async-done(((f32[8,8,8,128]{3,2,1,0:T(8,128)}), f32[8,8,8,128]{3,2,1,0:T(8,128)S(1)}, u32[]{:S(2)}, u32[]{:S(2)}) %all-to-all-start.4) | async-done | bytes 262176 | tf_op jit(solution)/shard_map/all_to_all | solution.py:30
  157.9 14.2 %all_to_all.33.sums_ref = f32[32,1,128]{2,1,0:T(1,128)S(1)} all-to-all(f32[32,1,128]{2,1,0:T(1,128)S(1)} %get-tuple-element.18), channel_id=1, replica_groups=mesh['row_0'=4,'row_1'=2,'row_2'=4,'col_0'=4,'col_1'=2] {'row_0','row_2'..., dimensions={0} | all-to-all | bytes 32768 | tf_op jit(solution)/shard_map/all_to_all | solution.py:30
  (52 shorter events, 12.7 us)
Async XLA Ops:
  0.6 0.7 copy-start.1
  35.1 18.5 %collective-permute-start = (f32[16,8,8,128]{3,2,1,0:T(8,128)S(1)}, f32[16,8,8,128]{3,2,1,0:T(8,128)S(1)}, u32[]{:S(2)}, u32[]{:S(2)}) collective-permute-start(f32[16,8,8,128]{3,2,1,0:T(8,128)S(1)} %all_to_all.31.own_ref), channel_id=1, source_target_pairs={{0,1},{1,0},{2,3},{3,2},{4,5},{5,4},{6,7},{7,6},{8,9},{9,8},{10,11... | collective-permute-start | bytes 1572872 | tf_op jit(solution)/shard_map/ppermute | solution.py:38
  38.4 10.6 %collective-permute-start.6 = (f32[64,256]{1,0:T(8,128)}, f32[64,256]{1,0:T(8,128)S(1)}, u32[]{:S(2)}, u32[]{:S(2)}) collective-permute-start(f32[64,256]{1,0:T(8,128)} %pv_hbm.1), channel_id=1, source_target_pairs={{0,0},{1,32},{2,64},{3,96},{4,128},{5,160},{6,192},{7,224},{8,8},{... | collective-permute-start | bytes 196616 | tf_op jit(solution)/shard_map/ppermute | solution.py:55
  40.7 8.3 %collective-permute-start.7 = (f32[64,256]{1,0:T(8,128)}, f32[64,256]{1,0:T(8,128)S(1)}, u32[]{:S(2)}, u32[]{:S(2)}) collective-permute-start(f32[64,256]{1,0:T(8,128)} %pv_hbm.1), channel_id=1, source_target_pairs={{0,32},{1,0},{2,96},{3,64},{4,160},{5,128},{6,224},{7,192},{8,40},... | collective-permute-start | bytes 196616 | tf_op jit(solution)/shard_map/ppermute | solution.py:55
  49.5 11.6 %collective-permute-start.8 = (f32[64,256]{1,0:T(8,128)S(1)}, f32[64,256]{1,0:T(8,128)S(1)}, u32[]{:S(2)}, u32[]{:S(2)}) collective-permute-start(f32[64,256]{1,0:T(8,128)S(1)} %get-tuple-element.14), channel_id=1, source_target_pairs={{8,0},{16,8},{24,16},{0,24},{9,1},{17,9},{25,17},{1,25},{10,2},{18... | collective-permute-start | bytes 196616 | tf_op jit(solution)/shard_map/ppermute | solution.py:42
  49.8 23.1 %collective-permute-start.20 = (f32[64,1280]{1,0:T(8,128)S(1)}, f32[64,1280]{1,0:T(8,128)S(1)}, u32[]{:S(2)}, u32[]{:S(2)}) collective-permute-start(f32[64,1280]{1,0:T(8,128)S(1)} %get-tuple-element.13.points_ref.refs_6_), channel_id=1, source_target_pairs={{2,0},{4,2},{6,4},{0,6},{3,1},{5,3},{7,5},{1,7},{10,8},{12,10},{14... | collective-permute-start | bytes 983048 | tf_op jit(solution)/shard_map/ppermute | solution.py:42
  53.6 30.8 %collective-permute-start.21 = (f32[64,1280]{1,0:T(8,128)S(1)}, f32[64,1280]{1,0:T(8,128)S(1)}, u32[]{:S(2)}, u32[]{:S(2)}) collective-permute-start(f32[64,1280]{1,0:T(8,128)S(1)} %get-tuple-element.13.points_ref.refs_6_), channel_id=1, source_target_pairs={{4,0},{6,2},{0,4},{2,6},{5,1},{7,3},{1,5},{3,7},{12,8},{14,10},{8,... | collective-permute-start | bytes 983048 | tf_op jit(solution)/shard_map/ppermute | solution.py:42
  55.6 32.0 %all-to-all-start.2 = ((f32[4,72,256]{2,1,0:T(8,128)}), f32[4,72,256]{2,1,0:T(8,128)S(1)}, u32[]{:S(2)}, u32[]{:S(2)}) async-start(f32[4,72,256]{2,1,0:T(8,128)} %shard_map.105), calls=%async_computation.2 | async-start | bytes 589824 | tf_op jit(solution)/shard_map/all_to_all | solution.py:30
  59.2 4.6 %collective-permute-start.9 = (f32[64,256]{1,0:T(8,128)S(1)}, f32[64,256]{1,0:T(8,128)S(1)}, u32[]{:S(2)}, u32[]{:S(2)}) collective-permute-start(f32[64,256]{1,0:T(8,128)S(1)} %get-tuple-element.14), channel_id=1, source_target_pairs={{16,0},{24,8},{0,16},{8,24},{17,1},{25,9},{1,17},{9,25},{18,2},{26... | collective-permute-start | bytes 196616 | tf_op jit(solution)/shard_map/ppermute | solution.py:42
  61.1 4.7 %collective-permute-start.10 = (f32[64,256]{1,0:T(8,128)S(1)}, f32[64,256]{1,0:T(8,128)S(1)}, u32[]{:S(2)}, u32[]{:S(2)}) collective-permute-start(f32[64,256]{1,0:T(8,128)S(1)} %get-tuple-element.14), channel_id=1, source_target_pairs={{24,0},{0,8},{8,16},{16,24},{25,1},{1,9},{9,17},{17,25},{26,2},{2,... | collective-permute-start | bytes 196616 | tf_op jit(solution)/shard_map/ppermute | solution.py:42
  61.1 6.6 %collective-permute-start.14 = (f32[64,256]{1,0:T(8,128)S(1)}, f32[64,256]{1,0:T(8,128)S(1)}, u32[]{:S(2)}, u32[]{:S(2)}) collective-permute-start(f32[64,256]{1,0:T(8,128)S(1)} %get-tuple-element.15), channel_id=1, source_target_pairs={{64,0},{128,64},{192,128},{0,192},{65,1},{129,65},{193,129},{1,193... | collective-permute-start | bytes 196616 | tf_op jit(solution)/shard_map/ppermute | solution.py:42
  63.8 21.3 %collective-permute-start.22 = (f32[64,1280]{1,0:T(8,128)S(1)}, f32[64,1280]{1,0:T(8,128)S(1)}, u32[]{:S(2)}, u32[]{:S(2)}) collective-permute-start(f32[64,1280]{1,0:T(8,128)S(1)} %get-tuple-element.13.points_ref.refs_6_), channel_id=1, source_target_pairs={{6,0},{0,2},{2,4},{4,6},{7,1},{1,3},{3,5},{5,7},{14,8},{8,10},{10,... | collective-permute-start | bytes 983048 | tf_op jit(solution)/shard_map/ppermute | solution.py:42
  65.8 4.6 %collective-permute-start.15 = (f32[64,256]{1,0:T(8,128)S(1)}, f32[64,256]{1,0:T(8,128)S(1)}, u32[]{:S(2)}, u32[]{:S(2)}) collective-permute-start(f32[64,256]{1,0:T(8,128)S(1)} %get-tuple-element.15), channel_id=1, source_target_pairs={{128,0},{192,64},{0,128},{64,192},{129,1},{193,65},{1,129},{65,193... | collective-permute-start | bytes 196616 | tf_op jit(solution)/shard_map/ppermute | solution.py:42
  67.7 4.6 %collective-permute-start.16 = (f32[64,256]{1,0:T(8,128)S(1)}, f32[64,256]{1,0:T(8,128)S(1)}, u32[]{:S(2)}, u32[]{:S(2)}) collective-permute-start(f32[64,256]{1,0:T(8,128)S(1)} %get-tuple-element.15), channel_id=1, source_target_pairs={{192,0},{0,64},{64,128},{128,192},{193,1},{1,65},{65,129},{129,193... | collective-permute-start | bytes 196616 | tf_op jit(solution)/shard_map/ppermute | solution.py:42
  70.4 18.6 %collective-permute-start.11 = (f32[4,64,256]{2,1,0:T(8,128)S(1)}, f32[4,64,256]{2,1,0:T(8,128)S(1)}, u32[]{:S(2)}, u32[]{:S(2)}) collective-permute-start(f32[4,64,256]{2,1,0:T(8,128)S(1)} %pad_maximum_fusion.refs_0_), channel_id=1, source_target_pairs={{64,0},{128,64},{192,128},{0,192},{65,1},{129,65},{193,129},{1,193... | collective-permute-start | bytes 786440 | tf_op jit(solution)/shard_map/ppermute | solution.py:42
  72.3 18.3 %collective-permute-start.12 = (f32[4,64,256]{2,1,0:T(8,128)S(1)}, f32[4,64,256]{2,1,0:T(8,128)S(1)}, u32[]{:S(2)}, u32[]{:S(2)}) collective-permute-start(f32[4,64,256]{2,1,0:T(8,128)S(1)} %pad_maximum_fusion.refs_0_), channel_id=1, source_target_pairs={{128,0},{192,64},{0,128},{64,192},{129,1},{193,65},{1,129},{65,193... | collective-permute-start | bytes 786440 | tf_op jit(solution)/shard_map/ppermute | solution.py:42
  72.9 17.6 %collective-permute-start.13 = (f32[4,64,256]{2,1,0:T(8,128)S(1)}, f32[4,64,256]{2,1,0:T(8,128)S(1)}, u32[]{:S(2)}, u32[]{:S(2)}) collective-permute-start(f32[4,64,256]{2,1,0:T(8,128)S(1)} %pad_maximum_fusion.refs_0_), channel_id=1, source_target_pairs={{192,0},{0,64},{64,128},{128,192},{193,1},{1,65},{65,129},{129,193... | collective-permute-start | bytes 786440 | tf_op jit(solution)/shard_map/ppermute | solution.py:42
  84.4 6.5 %collective-permute-start.17 = (f32[4,64,256]{2,1,0:T(8,128)S(1)}, f32[4,64,256]{2,1,0:T(8,128)S(1)}, u32[]{:S(2)}, u32[]{:S(2)}) collective-permute-start(f32[4,64,256]{2,1,0:T(8,128)S(1)} %pad_maximum_fusion.1.refs_4_), channel_id=1, source_target_pairs={{8,0},{16,8},{24,16},{0,24},{9,1},{17,9},{25,17},{1,25},{10,2},{18... | collective-permute-start | bytes 786440 | tf_op jit(solution)/shard_map/ppermute | solution.py:42
  87.5 12.1 %collective-permute-start.1 = (f32[4,72,256]{2,1,0:T(8,128)S(1)}, f32[4,72,256]{2,1,0:T(8,128)S(1)}, u32[]{:S(2)}, u32[]{:S(2)}) collective-permute-start(f32[4,72,256]{2,1,0:T(8,128)S(1)} %all-to-all-done.2.own_ref.rows_ref), channel_id=1, source_target_pairs={{0,1},{1,0},{2,3},{3,2},{4,5},{5,4},{6,7},{7,6},{8,9},{9,8},{10,11... | collective-permute-start | bytes 884744 | tf_op jit(solution)/shard_map/ppermute | solution.py:38
  88.9 9.4 %collective-permute-start.18 = (f32[4,64,256]{2,1,0:T(8,128)S(1)}, f32[4,64,256]{2,1,0:T(8,128)S(1)}, u32[]{:S(2)}, u32[]{:S(2)}) collective-permute-start(f32[4,64,256]{2,1,0:T(8,128)S(1)} %pad_maximum_fusion.1.refs_4_), channel_id=1, source_target_pairs={{16,0},{24,8},{0,16},{8,24},{17,1},{25,9},{1,17},{9,25},{18,2},{26... | collective-permute-start | bytes 786440 | tf_op jit(solution)/shard_map/ppermute | solution.py:42
  90.5 13.8 %collective-permute-start.19 = (f32[4,64,256]{2,1,0:T(8,128)S(1)}, f32[4,64,256]{2,1,0:T(8,128)S(1)}, u32[]{:S(2)}, u32[]{:S(2)}) collective-permute-start(f32[4,64,256]{2,1,0:T(8,128)S(1)} %pad_maximum_fusion.1.refs_4_), channel_id=1, source_target_pairs={{24,0},{0,8},{8,16},{16,24},{25,1},{1,9},{9,17},{17,25},{26,2},{2,... | collective-permute-start | bytes 786440 | tf_op jit(solution)/shard_map/ppermute | solution.py:42
  90.5 22.6 %collective-permute-start.23 = (f32[64,1280]{1,0:T(8,128)S(1)}, f32[64,1280]{1,0:T(8,128)S(1)}, u32[]{:S(2)}, u32[]{:S(2)}) collective-permute-start(f32[64,1280]{1,0:T(8,128)S(1)} %get-tuple-element.13.points_ref.refs_6_), channel_id=1, source_target_pairs={{0,1},{1,0},{2,3},{3,2},{4,5},{5,4},{6,7},{7,6},{8,9},{9,8},{10,11... | collective-permute-start | bytes 983048 | tf_op jit(solution)/shard_map/ppermute | solution.py:38
  90.9 23.7 %collective-permute-start.24 = (f32[64,1280]{1,0:T(8,128)S(1)}, f32[64,1280]{1,0:T(8,128)S(1)}, u32[]{:S(2)}, u32[]{:S(2)}) collective-permute-start(f32[64,1280]{1,0:T(8,128)S(1)} %collective-permute-done.20.refs_7_), channel_id=1, source_target_pairs={{0,1},{1,0},{2,3},{3,2},{4,5},{5,4},{6,7},{7,6},{8,9},{9,8},{10,11... | collective-permute-start | bytes 983048 | tf_op jit(solution)/shard_map/ppermute | solution.py:38
  98.3 21.2 %collective-permute-start.25 = (f32[64,1280]{1,0:T(8,128)S(1)}, f32[64,1280]{1,0:T(8,128)S(1)}, u32[]{:S(2)}, u32[]{:S(2)}) collective-permute-start(f32[64,1280]{1,0:T(8,128)S(1)} %collective-permute-done.21.refs_8_), channel_id=1, source_target_pairs={{0,1},{1,0},{2,3},{3,2},{4,5},{5,4},{6,7},{7,6},{8,9},{9,8},{10,11... | collective-permute-start | bytes 983048 | tf_op jit(solution)/shard_map/ppermute | solution.py:38
  99.7 19.9 %collective-permute-start.26 = (f32[64,1280]{1,0:T(8,128)S(1)}, f32[64,1280]{1,0:T(8,128)S(1)}, u32[]{:S(2)}, u32[]{:S(2)}) collective-permute-start(f32[64,1280]{1,0:T(8,128)S(1)} %collective-permute-done.22.refs_9_), channel_id=1, source_target_pairs={{0,1},{1,0},{2,3},{3,2},{4,5},{5,4},{6,7},{7,6},{8,9},{9,8},{10,11... | collective-permute-start | bytes 983048 | tf_op jit(solution)/shard_map/ppermute | solution.py:38
  104.3 8.8 %collective-permute-start.2 = (f32[4,128]{1,0:T(4,128)S(1)}, f32[4,128]{1,0:T(4,128)S(1)}, u32[]{:S(2)}, u32[]{:S(2)}) collective-permute-start(f32[4,128]{1,0:T(4,128)S(1)} %shard_map.106), channel_id=1, source_target_pairs={{0,0},{1,32},{2,64},{3,96},{4,128},{5,160},{6,192},{7,224},{8,8},{... | collective-permute-start | bytes 6152 | tf_op jit(solution)/shard_map/ppermute | solution.py:55
  113.1 6.4 %collective-permute-start.3 = (f32[4,128]{1,0:T(4,128)S(1)}, f32[4,128]{1,0:T(4,128)S(1)}, u32[]{:S(2)}, u32[]{:S(2)}) collective-permute-start(f32[4,128]{1,0:T(4,128)S(1)} %collective-permute-done.2.refs_0_), channel_id=1, source_target_pairs={{8,0},{16,8},{24,16},{0,24},{9,1},{17,9},{25,17},{1,25},{10,2},{18... | collective-permute-start | bytes 6152 | tf_op jit(solution)/shard_map/ppermute | solution.py:42
  113.1 6.4 %collective-permute-start.4 = (f32[4,128]{1,0:T(4,128)S(1)}, f32[4,128]{1,0:T(4,128)S(1)}, u32[]{:S(2)}, u32[]{:S(2)}) collective-permute-start(f32[4,128]{1,0:T(4,128)S(1)} %collective-permute-done.2.refs_0_), channel_id=1, source_target_pairs={{16,0},{24,8},{0,16},{8,24},{17,1},{25,9},{1,17},{9,25},{18,2},{26... | collective-permute-start | bytes 6152 | tf_op jit(solution)/shard_map/ppermute | solution.py:42
  114.6 4.9 %collective-permute-start.5 = (f32[4,128]{1,0:T(4,128)S(1)}, f32[4,128]{1,0:T(4,128)S(1)}, u32[]{:S(2)}, u32[]{:S(2)}) collective-permute-start(f32[4,128]{1,0:T(4,128)S(1)} %collective-permute-done.2.refs_0_), channel_id=1, source_target_pairs={{24,0},{0,8},{8,16},{16,24},{25,1},{1,9},{9,17},{17,25},{26,2},{2,... | collective-permute-start | bytes 6152 | tf_op jit(solution)/shard_map/ppermute | solution.py:42
  119.5 52.6 %copy-start = (f32[1,8,128]{2,1,0:T(8,128)S(1)}, f32[1,8,128]{2,1,0:T(8,128)}, u32[]{:S(2)}) copy-start(f32[1,8,128]{2,1,0:T(8,128)} %param.9) | copy-start | bytes 12292
  123.6 2.0 %collective-permute-start.27 = (f32[16,8,8,128]{3,2,1,0:T(8,128)S(1)}, f32[16,8,8,128]{3,2,1,0:T(8,128)S(1)}, u32[]{:S(2)}, u32[]{:S(2)}) collective-permute-start(f32[16,8,8,128]{3,2,1,0:T(8,128)S(1)} %get-tuple-element.17), channel_id=1, source_target_pairs={{0,1},{1,0},{2,3},{3,2},{4,5},{5,4},{6,7},{7,6},{8,9},{9,8},{10,11... | collective-permute-start | bytes 1572872 | tf_op jit(solution)/shard_map/ppermute | solution.py:38
  144.1 13.6 %all-to-all-start.4 = ((f32[8,8,8,128]{3,2,1,0:T(8,128)}), f32[8,8,8,128]{3,2,1,0:T(8,128)S(1)}, u32[]{:S(2)}, u32[]{:S(2)}) async-start(f32[8,8,8,128]{3,2,1,0:T(8,128)} %shard_map.111), calls=%async_computation.4 | async-start | bytes 524288 | tf_op jit(solution)/shard_map/all_to_all | solution.py:30
